TPU v7x, 32 devices: a whole 2x2x4 slice. The times are simulated.
32 devices in a mesh: tp: 4 (over z), fsdp: 8 (over y, x, core).
Axes of the slice: x: 2, y: 2, z: 4, core: 2. Of those that a mesh axis runs over, the one named last changes fastest.
Arguments:
- resid_in: bfloat16 [8, 1536, 5120], P('fsdp', 'tp')
- grad_out: bfloat16 [8, 1536, 5120], P('fsdp', 'tp')
- norm_gain: float32 [5120], replicated
- w_qkv: bfloat16 [5120, 7168], P('fsdp', 'tp')
- b_qkv: bfloat16 [7168], P('tp')
- sinks: float32 [40], P('tp')
- w_out: bfloat16 [5120, 5120], P(('tp', 'fsdp'))
- b_out: bfloat16 [5120], replicated
Outputs:
- output 1: bfloat16 [8, 1536, 5120], P('fsdp', 'tp')
- output 2: bfloat16 [8, 1536, 5120], P('fsdp', 'tp')
- output 3: float32 [5120], replicated
- output 4: float32 [5120, 7168], P('fsdp', 'tp')
- output 5: float32 [7168], P('tp')
- output 6: float32 [40], P('tp')
- output 7: float32 [5120, 5120], P(('tp', 'fsdp'))
- output 8: float32 [5120], replicated
All inputs are finite; a program needn't handle non-finite values.
Results may differ from a plain program's by a relative error of at most 0.0108997.
Values are sent between devices in bfloat16 or wider.
A program may use at most 1 GiB of HBM per device.

v0:
```python
import jax
import jax.numpy as jnp
from jax import lax
from jax.sharding import PartitionSpec as P

EPS = 1e-5
ROPE_BASE = 150000.0
WINDOW = 128


def rope_tables(positions, head_dim):
    inv_freq = ROPE_BASE ** (-2.0 * jnp.arange(head_dim // 2).astype(jnp.float32) / head_dim)
    angles = positions.astype(jnp.float32)[:, None] * inv_freq[None, :]
    return jnp.cos(angles), jnp.sin(angles)


def apply_rope(head_vals, cos_tab, sin_tab):
    half_dim = head_vals.shape[-1] // 2
    first_half = head_vals[..., :half_dim]
    second_half = head_vals[..., half_dim:]
    return jnp.concatenate([first_half * cos_tab - second_half * sin_tab, second_half * cos_tab + first_half * sin_tab], axis=-1)


def rope_back(head_grads, cos_tab, sin_tab):
    half_dim = head_grads.shape[-1] // 2
    first_half = head_grads[..., :half_dim]
    second_half = head_grads[..., half_dim:]
    return jnp.concatenate([first_half * cos_tab + second_half * sin_tab, second_half * cos_tab - first_half * sin_tab], axis=-1)


def split_qkv(qkv_proj, positions, kv_count, head_dim):
    n_rows, seq_len = qkv_proj.shape[0], qkv_proj.shape[1]
    grouped = qkv_proj.reshape(n_rows, seq_len, kv_count, -1, head_dim)
    group_size = grouped.shape[3] - 2
    cos_tab, sin_tab = rope_tables(positions, head_dim)
    queries = apply_rope(grouped[:, :, :, :group_size].astype(jnp.float32), cos_tab[:, None, None], sin_tab[:, None, None])
    keys_rot = apply_rope(grouped[:, :, :, group_size].astype(jnp.float32), cos_tab[:, None], sin_tab[:, None])
    return queries.astype(jnp.bfloat16), keys_rot.astype(jnp.bfloat16), grouped[:, :, :, group_size + 1]


def band_mask(first_pos, blk_start):
    q_idx = jnp.arange(WINDOW)[:, None]
    k_idx = jnp.arange(2 * WINDOW)[None, :]
    return (k_idx > q_idx) & (k_idx <= q_idx + WINDOW) & (first_pos + blk_start - WINDOW + k_idx >= 0)


def block_scores(q_blk, k_blk, first_pos, blk_start):
    qk_scale = q_blk.shape[-1] ** -0.5
    scores = jnp.einsum("niegd,njed->negij", q_blk, k_blk, preferred_element_type=jnp.float32) * qk_scale
    return jnp.where(band_mask(first_pos, blk_start), scores, -1e30)


def attend_forward(queries, keys_ext, values_ext, sink_loc, first_pos):
    n_rows, q_len, kv_loc, group_size, head_dim = queries.shape
    sink_col = sink_loc.reshape(1, kv_loc, group_size, 1)

    def block_body(block_idx, loop_carry):
        out_acc, norm_acc = loop_carry
        blk_start = block_idx * WINDOW
        q_blk = lax.dynamic_slice_in_dim(queries, blk_start, WINDOW, axis=1)
        k_blk = lax.dynamic_slice_in_dim(keys_ext, blk_start, 2 * WINDOW, axis=1)
        v_blk = lax.dynamic_slice_in_dim(values_ext, blk_start, 2 * WINDOW, axis=1)
        scores = block_scores(q_blk, k_blk, first_pos, blk_start)
        row_max = jnp.maximum(jnp.max(scores, axis=-1), sink_col)
        exp_scores = jnp.exp(scores - row_max[..., None])
        row_denom = jnp.sum(exp_scores, axis=-1) + jnp.exp(sink_col - row_max)
        attn_probs = (exp_scores / row_denom[..., None]).astype(jnp.bfloat16)
        out_blk = jnp.einsum("negij,njed->niegd", attn_probs, v_blk, preferred_element_type=jnp.float32)
        out_acc = lax.dynamic_update_slice_in_dim(out_acc, out_blk.astype(jnp.bfloat16), blk_start, axis=1)
        norm_acc = lax.dynamic_update_slice_in_dim(norm_acc, row_max + jnp.log(row_denom), blk_start, axis=3)
        return out_acc, norm_acc

    init_carry = (jnp.zeros(queries.shape, jnp.bfloat16), jnp.zeros((n_rows, kv_loc, group_size, q_len), jnp.float32))
    return lax.fori_loop(0, q_len // WINDOW, block_body, init_carry)


def attend_backward(queries, keys_ext, values_ext, sink_loc, first_pos, log_norm, d_out):
    n_rows, q_len, kv_loc, group_size, head_dim = queries.shape
    qk_scale = head_dim ** -0.5
    sink_col = sink_loc.reshape(1, kv_loc, group_size, 1)

    def block_body(block_idx, loop_carry):
        dq_acc, dk_acc, dv_acc, dsink_acc = loop_carry
        blk_start = block_idx * WINDOW
        q_blk = lax.dynamic_slice_in_dim(queries, blk_start, WINDOW, axis=1)
        k_blk = lax.dynamic_slice_in_dim(keys_ext, blk_start, 2 * WINDOW, axis=1)
        v_blk = lax.dynamic_slice_in_dim(values_ext, blk_start, 2 * WINDOW, axis=1)
        do_blk = lax.dynamic_slice_in_dim(d_out, blk_start, WINDOW, axis=1)
        norm_blk = lax.dynamic_slice_in_dim(log_norm, blk_start, WINDOW, axis=3)
        attn_probs = jnp.exp(block_scores(q_blk, k_blk, first_pos, blk_start) - norm_blk[..., None])
        dv_blk = jnp.einsum("negij,niegd->njed", attn_probs.astype(jnp.bfloat16), do_blk, preferred_element_type=jnp.float32)
        d_probs = jnp.einsum("niegd,njed->negij", do_blk, v_blk, preferred_element_type=jnp.float32).astype(jnp.bfloat16).astype(jnp.float32)
        row_dot = jnp.sum(attn_probs * d_probs, axis=-1)
        d_scores = (attn_probs * (d_probs - row_dot[..., None])).astype(jnp.bfloat16)
        sink_probs = jnp.exp(sink_col - norm_blk)
        dsink_acc = dsink_acc - jnp.sum(sink_probs * row_dot, axis=(0, 3))
        dq_blk = jnp.einsum("negij,njed->niegd", d_scores, k_blk, preferred_element_type=jnp.float32) * qk_scale
        dk_blk = jnp.einsum("negij,niegd->njed", d_scores, q_blk, preferred_element_type=jnp.float32) * qk_scale
        dq_acc = lax.dynamic_update_slice_in_dim(dq_acc, dq_blk.astype(jnp.bfloat16), blk_start, axis=1)
        dk_acc = lax.dynamic_update_slice_in_dim(dk_acc, lax.dynamic_slice_in_dim(dk_acc, blk_start, 2 * WINDOW, axis=1) + dk_blk, blk_start, axis=1)
        dv_acc = lax.dynamic_update_slice_in_dim(dv_acc, lax.dynamic_slice_in_dim(dv_acc, blk_start, 2 * WINDOW, axis=1) + dv_blk, blk_start, axis=1)
        return dq_acc, dk_acc, dv_acc, dsink_acc

    init_carry = (jnp.zeros(queries.shape, jnp.bfloat16), jnp.zeros(keys_ext.shape, jnp.float32), jnp.zeros(values_ext.shape, jnp.float32), jnp.zeros((kv_loc, group_size), jnp.float32))
    dq_all, dk_all, dv_all, dsink_all = lax.fori_loop(0, q_len // WINDOW, block_body, init_carry)
    return dq_all, dk_all, dv_all, dsink_all.reshape(-1)


def norm_backward(d_normed, resid_f32, inv_rms, norm_gain, grad_loc):
    d_normed = d_normed.astype(jnp.bfloat16).astype(jnp.float32)
    gain_grad = d_normed * norm_gain
    d_resid = inv_rms * (gain_grad - resid_f32 * inv_rms * inv_rms * jnp.mean(gain_grad * resid_f32, axis=-1, keepdims=True))
    grad_resid = (grad_loc.astype(jnp.float32) + d_resid).astype(jnp.bfloat16)
    grad_gain = jnp.sum(d_normed * resid_f32 * inv_rms, axis=(0, 1))
    return grad_resid, grad_gain


def solution(mesh):
    act_spec = P("fsdp", "tp", None)
    wout_spec = P(("tp", "fsdp"), None)
    in_specs = (act_spec, act_spec, P(), P("fsdp", "tp"), P("tp"), P("tp"), wout_spec, P())
    out_specs = (act_spec, act_spec, P(), P("fsdp", "tp"), P("tp"), P("tp"), wout_spec, P())

    def device_step(resid_loc, grad_loc, norm_gain, wqkv_loc, bqkv_loc, sink_loc, wout_loc, b_out):
        n_rows = resid_loc.shape[0]
        heads_loc = sink_loc.shape[0]
        resid_f32 = resid_loc.astype(jnp.float32)
        inv_rms = lax.rsqrt(jnp.mean(resid_f32 * resid_f32, axis=-1, keepdims=True) + EPS)
        normed = (resid_f32 * inv_rms * norm_gain).astype(jnp.bfloat16)

        wqkv_full = lax.all_gather(wqkv_loc, "fsdp", axis=0, tiled=True)
        wout_full = lax.all_gather(wout_loc, "fsdp", axis=0, tiled=True)
        normed_all = lax.all_gather(normed, "tp", axis=1, tiled=True)
        seq_len = normed_all.shape[1]
        head_dim = wout_full.shape[0] // heads_loc
        kv_loc = (wqkv_full.shape[1] // head_dim - heads_loc) // 2

        qkv_proj = (jnp.dot(normed_all, wqkv_full, preferred_element_type=jnp.float32) + bqkv_loc.astype(jnp.float32)).astype(jnp.bfloat16)
        positions = jnp.arange(seq_len)
        queries, keys_rot, values = split_qkv(qkv_proj, positions, kv_loc, head_dim)
        pad_zeros = jnp.zeros((n_rows, WINDOW, kv_loc, head_dim), jnp.bfloat16)
        keys_ext = jnp.concatenate([pad_zeros, keys_rot], axis=1)
        values_ext = jnp.concatenate([pad_zeros, values], axis=1)
        attn_out, log_norm = attend_forward(queries, keys_ext, values_ext, sink_loc, 0)
        attn_flat = attn_out.reshape(n_rows, seq_len, heads_loc * head_dim)
        part_sum = jnp.dot(attn_flat, wout_full, preferred_element_type=jnp.float32)
        proj_out = lax.psum_scatter(part_sum, "tp", scatter_dimension=1, tiled=True)
        resid_out = (resid_f32 + proj_out + b_out.astype(jnp.float32)).astype(jnp.bfloat16)

        grad_bout = lax.psum(jnp.sum(grad_loc, axis=(0, 1), dtype=jnp.float32), ("fsdp", "tp"))
        grad_all = lax.all_gather(grad_loc, "tp", axis=1, tiled=True)
        wout_part = jnp.einsum("nth,ntk->hk", attn_flat, grad_all, preferred_element_type=jnp.float32)
        grad_wout = lax.psum_scatter(wout_part, "fsdp", scatter_dimension=0, tiled=True)
        d_attn = jnp.einsum("ntk,hk->nth", grad_all, wout_full, preferred_element_type=jnp.float32).astype(jnp.bfloat16)
        dq_rot, dk_ext, dv_ext, sink_part = attend_backward(queries, keys_ext, values_ext, sink_loc, 0, log_norm, d_attn.reshape(attn_out.shape))
        cos_tab, sin_tab = rope_tables(positions, head_dim)
        d_query = rope_back(dq_rot.astype(jnp.float32), cos_tab[:, None, None], sin_tab[:, None, None]).astype(jnp.bfloat16)
        d_key = rope_back(dk_ext[:, WINDOW:].astype(jnp.bfloat16).astype(jnp.float32), cos_tab[:, None], sin_tab[:, None]).astype(jnp.bfloat16)
        d_value = dv_ext[:, WINDOW:].astype(jnp.bfloat16)
        d_qkv = jnp.concatenate([d_query, d_key[:, :, :, None], d_value[:, :, :, None]], axis=3).reshape(qkv_proj.shape)
        wqkv_part = jnp.einsum("ntd,ntc->dc", normed_all, d_qkv, preferred_element_type=jnp.float32)
        grad_wqkv = lax.psum_scatter(wqkv_part, "fsdp", scatter_dimension=0, tiled=True)
        grad_bqkv = lax.psum(jnp.sum(d_qkv, axis=(0, 1), dtype=jnp.float32), "fsdp")
        grad_sinks = lax.psum(sink_part, "fsdp")
        normed_part = jnp.einsum("ntc,dc->ntd", d_qkv, wqkv_full, preferred_element_type=jnp.float32)
        d_normed = lax.psum_scatter(normed_part, "tp", scatter_dimension=1, tiled=True)
        grad_resid, gain_part = norm_backward(d_normed, resid_f32, inv_rms, norm_gain, grad_loc)
        grad_gain = lax.psum(gain_part, ("fsdp", "tp"))
        return (resid_out, grad_resid, grad_gain, grad_wqkv, grad_bqkv, grad_sinks, grad_wout, grad_bout)

    return jax.shard_map(device_step, mesh=mesh, in_specs=in_specs, out_specs=out_specs, check_vma=False)
```

profile of v0, /device:TPU:0, one launch (start us, length us, event | category | flops | bytes accessed | tf_op | source)
XLA Modules:
  0.0 2418.7 jit_solution(8714547432716526218)
XLA Ops:
  8.7 3.1 fusion.78
  12.4 3.2 fusion.74
  17.9 68.9 %all-gather.9.cloned.1.call-done = bf16[1280,5120]{1,0:T(8,128)(2,1)} async-done(((bf16[160,5120]{1,0:T(8,128)(2,1)}), bf16[1280,5120]{1,0:T(8,128)(2,1)}) %all-gather.9.cloned.1.call-update) | async-done | bytes 13107216 | tf_op jit(solution)/shard_map/all_gather | solution.py:132
  86.7 272.1 %all-gather.11.cloned.1.call-done = bf16[1,1536,5120]{2,1,0:T(8,128)(2,1)} async-done(((bf16[1,384,5120]{2,1,0:T(8,128)(2,1)}), bf16[1,1536,5120]{2,1,0:T(8,128)(2,1)}) %all-gather.11.cloned.1.call-update) | async-done | bytes 15728656 | tf_op jit(solution)/shard_map/all_gather | solution.py:151
  358.8 28.9 %fusion.84 = bf16[1536,1280]{0,1:T(8,128)(2,1)} fusion(bf16[1280,5120]{1,0:T(8,128)(2,1)} %all-gather.9.cloned.1.call-done, bf16[1,1536,5120]{2,1,0:T(8,128)(2,1)} %all-gather.11.cloned.1.call-done), kind=kOutput, calls=%fused_computation.120 | convolution fusion | flops 20134625280 | bytes 32768000 | tf_op jit(solution)/shard_map/ntk,hk->nth/dot_general | solution.py:154
  387.7 241.9 %all-gather.5.cloned.1.call-done = bf16[1,1536,5120]{2,1,0:T(8,128)(2,1)} async-done(((bf16[1,384,5120]{2,1,0:T(8,128)(2,1)}), bf16[1,1536,5120]{2,1,0:T(8,128)(2,1)}) %all-gather.5.cloned.1.call-update) | async-done | bytes 15728656 | tf_op jit(solution)/shard_map/all_gather | solution.py:133
  629.6 96.2 %all-gather.7.cloned.1.call-done = bf16[5120,1792]{1,0:T(8,128)(2,1)} async-done(((bf16[640,1792]{1,0:T(8,128)(2,1)}), bf16[5120,1792]{1,0:T(8,128)(2,1)}) %all-gather.7.cloned.1.call-update) | async-done | bytes 18350096 | tf_op jit(solution)/shard_map/all_gather | solution.py:131
  725.9 37.6 %add_convert_fusion = bf16[1536,1792]{1,0:T(8,128)(2,1)} fusion(bf16[5120,1792]{1,0:T(8,128)(2,1)} %all-gather.7.cloned.1.call-done, bf16[1,1536,5120]{2,1,0:T(8,128)(2,1)} %all-gather.5.cloned.1.call-done, f32[1792]{0:T(1024)S(1)} %convert_element_type.292), kind=kOutput, calls=%fused_computation.103 | convolution fusion | flops 28191227904 | bytes 39590912 | tf_op jit(solution)/shard_map/dot_general | solution.py:138
  763.4 8.4 copy.43
  771.8 2.4 fusion.89
  774.3 6.3 slice_convert_fusion
  781.2 4.6 subtract_convert_fusion.1
  785.8 2.2 pad_maximum_fusion.2
  788.0 6.3 copy.46
  795.5 2.3 broadcast.336.clone
  797.7 47.1 %while.39 = (s32[]{:T(128)}, bf16[1,1536,2,5,128]{1,4,3,2,0:T(8,128)(2,1)}, f32[1,2,5,1536]{3,2,1,0:T(8,128)S(1)}, bf16[1,1664,2,128]{1,3,2,0:T(8,128)(2,1)}, bf...) while((s32[]{:T(128)}, ...), condition=%wide.region_4.5_spmd, body=%wide.region_1.4_spmd.sunk | while | flops 170696832 | bytes 4993848 | solution.py:74
  799.6 2.0 fusion.129
  807.5 2.0 fusion.129
  815.3 2.0 fusion.129
  823.2 2.0 fusion.129
  838.9 2.0 fusion.129
  846.3 2.3 broadcast.336
  848.5 96.0 %while.40 = (s32[]{:T(128)}, bf16[1,1536,2,5,128]{1,4,3,2,0:T(8,128)(2,1)}, f32[1,1664,2,128]{1,3,2,0:T(8,128)S(1)}, f32[1,1664,2,128]{1,3,2,0:T(8,128)}, f32[2,...) while((s32[]{:T(128)}, ...), condition=%wide.region_9.10_spmd.clone, body=%wide.region_6.9_spmd.clone.sunk | while | flops 424021152 | bytes 11051006 | solution.py:105
  852.0 2.1 fusion.145
  860.0 2.1 fusion.145
  868.0 2.1 fusion.145
  876.0 2.1 fusion.145
  884.0 2.1 fusion.145
  892.0 2.1 fusion.145
  900.0 2.1 fusion.145
  908.0 2.1 fusion.145
  916.0 2.1 fusion.145
  924.0 2.1 fusion.145
  932.0 2.1 fusion.145
  940.0 2.1 fusion.145
  951.4 2.4 copy-done.7
  953.9 34.8 %convolution_bitcast_fusion.2 = f32[1,1536,5120]{2,1,0:T(8,128)} fusion(bf16[1536,1792]{0,1:T(8,128)(2,1)S(1)} %bitcast.269, bf16[5120,1792]{1,0:T(8,128)(2,1)} %all-gather.7.cloned.1.call-done), kind=kOutput, calls=%fused_computation.87 | convolution fusion | flops 28185722880 | bytes 55312384 | tf_op jit(solution)/shard_map/ntc,dc->ntd/dot_general | solution.py:165
  988.7 27.6 %convolution_bitcast_fusion.3 = f32[1,1536,5120]{2,1,0:T(8,128)} fusion(bf16[1536,1280]{0,1:T(8,128)(2,1)} %bitcast.271, bf16[1280,5120]{1,0:T(8,128)(2,1)} %all-gather.9.cloned.1.call-done), kind=kOutput, calls=%fused_computation.88 | convolution fusion | flops 20132659200 | bytes 48496640 | tf_op jit(solution)/shard_map/dot_general | solution.py:146
  1016.4 27.5 %fusion.61 = f32[1280,5120]{1,0:T(8,128)} fusion(bf16[1536,1280]{0,1:T(8,128)(2,1)} %bitcast.272, bf16[1,1536,5120]{2,1,0:T(8,128)(2,1)} %all-gather.11.cloned.1.call-done), kind=kOutput, calls=%fused_computation.89 | convolution fusion | flops 20132659200 | bytes 45875200 | tf_op jit(solution)/shard_map/nth,ntk->hk/dot_general | solution.py:152
  1044.0 36.2 %fusion.65 = f32[5120,1792]{1,0:T(8,128)} fusion(bf16[1536,1792]{0,1:T(8,128)(2,1)} %bitcast.270, bf16[1,1536,5120]{2,1,0:T(8,128)(2,1)} %all-gather.5.cloned.1.call-done), kind=kOutput, calls=%fused_computation.93 | convolution fusion | flops 28185722880 | bytes 57933824 | tf_op jit(solution)/shard_map/ntd,ntc->dc/dot_general | solution.py:161
  1085.0 14.7 all-reduce.3
  1099.7 404.2 %reduce-scatter.7.cloned.1.call-done = f32[1,384,5120]{2,1,0:T(8,128)} async-done(((f32[1,1536,5120]{2,1,0:T(8,128)}), f32[1,384,5120]{2,1,0:T(8,128)}) %reduce-scatter.7.cloned.1.call-update) | async-done | bytes 7864336 | tf_op jit(solution)/shard_map/reduce_scatter | solution.py:166
  1503.9 5.6 fusion.83
  1509.5 513.1 %reduce-scatter.5.cloned.1.call-done = f32[1,384,5120]{2,1,0:T(8,128)} async-done(((f32[1,1536,5120]{2,1,0:T(8,128)}), f32[1,384,5120]{2,1,0:T(8,128)}) %reduce-scatter.5.cloned.1.call-update) | async-done | bytes 7864336 | tf_op jit(solution)/shard_map/reduce_scatter | solution.py:147
  2022.6 12.4 convert_reduce_fusion.1
  2035.0 42.2 %all-reduce.2 = (f32[5120]{0:T(1024)}, f32[5120]{0:T(1024)}) all-reduce(f32[5120]{0:T(1024)S(1)} %get-tuple-element.530, f32[5120]{0:T(1024)S(1)} %get-tuple-element.582), channel_id=1, replica_groups=mesh['tp'=4,'fsdp'=8] {'fsdp','tp'}, use_global_device_ids=true, to_apply=%region_13.14 | all-reduce | flops 10240 | bytes 81920 | tf_op jit(solution)/shard_map/psum | solution.py:168
  2077.2 111.0 %reduce-scatter.11.cloned.1.call-done = f32[160,5120]{1,0:T(8,128)} async-done(((f32[1280,5120]{1,0:T(8,128)}), f32[160,5120]{1,0:T(8,128)}) %reduce-scatter.11.cloned.1.call-update) | async-done | bytes 3276816 | tf_op jit(solution)/shard_map/reduce_scatter | solution.py:153
  2188.2 223.4 %reduce-scatter.9.cloned.1.call-done = f32[640,1792]{1,0:T(8,128)} async-done(((f32[5120,1792]{1,0:T(8,128)}), f32[640,1792]{1,0:T(8,128)}) %reduce-scatter.9.cloned.1.call-update) | async-done | bytes 4587536 | tf_op jit(solution)/shard_map/reduce_scatter | solution.py:162
  (323 shorter events, 125.8 us)
Async XLA Ops:
  7.2 79.6 %all-gather.9.cloned.1.call-start = ((), (), s32[]{:S(2)}) async-start(), calls=%async_computation.6 | async-start | bytes 14745600 | tf_op jit(solution)/shard_map/all_gather | solution.py:132
  7.9 4.5 copy-start.13
  7.9 350.9 %all-gather.11.cloned.1.call-start = ((), (), s32[]{:S(2)}) async-start(), calls=%async_computation.8 | async-start | bytes 19660800 | tf_op jit(solution)/shard_map/all_gather | solution.py:151
  8.7 621.0 %all-gather.5.cloned.1.call-start = ((), (), s32[]{:S(2)}) async-start(), calls=%async_computation.4 | async-start | bytes 19660800 | tf_op jit(solution)/shard_map/all_gather | solution.py:133
  8.7 3.7 copy-start
  11.8 0.6 copy-start.15
  15.6 0.7 copy-start.21
  15.6 0.8 copy-start.20
  15.7 710.2 %all-gather.7.cloned.1.call-start = ((), (), s32[]{:S(2)}) async-start(), calls=%async_computation.5 | async-start | bytes 20643840 | tf_op jit(solution)/shard_map/all_gather | solution.py:131
  16.2 1487.7 %reduce-scatter.7.cloned.1.call-start = ((), (), s32[]{:S(2)}) async-start(), calls=%async_computation.9 | async-start | bytes 39321600 | tf_op jit(solution)/shard_map/reduce_scatter | solution.py:166
  788.0 6.4 copy-start.12
  944.5 3.7 copy-start.17
  944.5 2.6 copy-start.4
  946.2 3.4 copy-start.5
  946.7 2.9 copy-start.8
  946.7 2.9 copy-start.10
  949.5 1.4 copy-start.1
  949.5 1.9 copy-start.3
  951.4 2.4 copy-start.7
  988.6 1034.0 %reduce-scatter.5.cloned.1.call-start = ((), (), s32[]{:S(2)}) async-start(), calls=%async_computation.7 | async-start | bytes 39321600 | tf_op jit(solution)/shard_map/reduce_scatter | solution.py:147
  1016.3 1171.9 %reduce-scatter.11.cloned.1.call-start = ((), (), s32[]{:S(2)}) async-start(), calls=%async_computation.11 | async-start | bytes 29491200 | tf_op jit(solution)/shard_map/reduce_scatter | solution.py:153
  1044.0 1367.7 %reduce-scatter.9.cloned.1.call-start = ((), (), s32[]{:S(2)}) async-start(), calls=%async_computation.10 | async-start | bytes 41287680 | tf_op jit(solution)/shard_map/reduce_scatter | solution.py:162
  1080.2 0.7 copy-start.19
  1080.2 0.7 copy-start.18
  1080.2 1.0 copy-start.9
  1080.2 1.1 copy-start.11
  1080.2 1.8 copy-start.2
  1082.1 1.9 copy-start.6
  1083.9 420.0 %copy-start.14 = (f32[5120]{0:T(1024)S(1)}, f32[5120]{0:T(1024)}, u32[]{:S(2)}) copy-start(f32[5120]{0:T(1024)} %param.14) | copy-start | bytes 61444
  1084.0 420.0 %copy-start.16 = (f32[384]{0:T(512)S(1)}, f32[384]{0:T(512)}, u32[]{:S(2)}) copy-start(f32[384]{0:T(512)} %copy-done.15) | copy-start | bytes 4612
Sparse Core Ops, SparseCore 0:
  9.9 76.8 all-gather.8
  88.3 270.4 all-gather.10
  361.0 268.6 all-gather.4
  631.4 94.4 all-gather.6
  988.8 515.1 reduce-scatter.6
  1506.1 516.4 reduce-scatter.4
  2026.9 161.3 reduce-scatter.10
  2192.5 219.0 reduce-scatter.8
where the time goes:
time: 2420 us
  waiting for transfers between devices  1930 us (80%)
  matrix products  323 us (13%)
  other arithmetic  59.9 us (2%)
  blocking collectives  57 us (2%)
  local copies, waits for them, and re-layouts  30.5 us (1%)
    reduce_scatter x1, waiting for transfers between devices, device_step(): proj_out = lax.psum_scatter(part_sum, 'tp', scatter_dimension=1, tiled=True)  513 us
    reduce_scatter x1, waiting for transfers between devices, device_step(): lax.psum_scatter(normed_part, 'tp', scatter_dimension=1, tiled=True)  404 us
    all_gather x1, waiting for transfers between devices, device_step(): grad_all = lax.all_gather(grad_loc, 'tp', axis=1, tiled=True)  272 us
    all_gather x1, waiting for transfers between devices, device_step(): normed_all = lax.all_gather(normed, 'tp', axis=1, tiled=True)  242 us
    reduce_scatter x1, waiting for transfers between devices, device_step(): lax.psum_scatter(wqkv_part, 'fsdp', scatter_dimension=0, tiled=True)  223 us
    reduce_scatter x1, waiting for transfers between devices, device_step(): lax.psum_scatter(wout_part, 'fsdp', scatter_dimension=0, tiled=True)  111 us
    all_gather x1, waiting for transfers between devices, device_step(): wqkv_full = lax.all_gather(wqkv_loc, 'fsdp', axis=0, tiled=True)  96.2 us
    all_gather x1, waiting for transfers between devices, device_step(): wout_full = lax.all_gather(wout_loc, 'fsdp', axis=0, tiled=True)  68.9 us
  transfers between devices with their start and end apart: 8, of which 8 were waited for; matrix products, arithmetic and copies ran while one was open for 6% of the time, Pallas kernels for 0%

commit v1 on v0

--- a/solution.py
+++ b/solution.py
@@ -2,6 +2,7 @@
 import jax.numpy as jnp
 from jax import lax
 from jax.sharding import PartitionSpec as P
+
 
 EPS = 1e-5
 ROPE_BASE = 150000.0
@@ -51,7 +52,7 @@
 
 
 def attend_forward(queries, keys_ext, values_ext, sink_loc, first_pos):
-    n_rows, q_len, kv_loc, group_size, head_dim = queries.shape
+    n_rows, q_len, kv_loc, group_size, _ = queries.shape
     sink_col = sink_loc.reshape(1, kv_loc, group_size, 1)
 
     def block_body(block_idx, loop_carry):
@@ -75,7 +76,7 @@
 
 
 def attend_backward(queries, keys_ext, values_ext, sink_loc, first_pos, log_norm, d_out):
-    n_rows, q_len, kv_loc, group_size, head_dim = queries.shape
+    _, q_len, kv_loc, group_size, head_dim = queries.shape
     qk_scale = head_dim ** -0.5
     sink_col = sink_loc.reshape(1, kv_loc, group_size, 1)
 
@@ -115,57 +116,129 @@
     return grad_resid, grad_gain
 
 
+def ordered(value, *earlier):
+    return lax.optimization_barrier((value, earlier))[0]
+
+
+def tp_shift(value, step, n_ranks):
+    return lax.ppermute(value, "tp", [(rank, (rank + step) % n_ranks) for rank in range(n_ranks)])
+
+
+def ring_gather(shard, n_ranks, *earlier):
+    pieces = [shard]
+    held = ordered(shard, *earlier) if earlier else shard
+    for _ in range(n_ranks - 1):
+        held = tp_shift(held, 1, n_ranks)
+        pieces.append(held)
+    return pieces
+
+
+def exchange(pieces_by_dest, n_ranks):
+    received = [pieces_by_dest[0]]
+    for step in range(1, n_ranks):
+        received.append(tp_shift(pieces_by_dest[step], step, n_ranks))
+    return received
+
+
 def solution(mesh):
     act_spec = P("fsdp", "tp", None)
     wout_spec = P(("tp", "fsdp"), None)
     in_specs = (act_spec, act_spec, P(), P("fsdp", "tp"), P("tp"), P("tp"), wout_spec, P())
     out_specs = (act_spec, act_spec, P(), P("fsdp", "tp"), P("tp"), P("tp"), wout_spec, P())
+    n_tp = mesh.shape["tp"]
+    n_fsdp = mesh.shape["fsdp"]
 
     def device_step(resid_loc, grad_loc, norm_gain, wqkv_loc, bqkv_loc, sink_loc, wout_loc, b_out):
-        n_rows = resid_loc.shape[0]
+        n_rows, loc_len, _ = resid_loc.shape
         heads_loc = sink_loc.shape[0]
+        rank = lax.axis_index("tp")
+        seq_len = loc_len * n_tp
+        head_dim = wout_loc.shape[0] * n_fsdp // heads_loc
+        kv_loc = (wqkv_loc.shape[1] // head_dim - heads_loc) // 2
+        out_loc = heads_loc * head_dim
+
+        def chunk_of(arr, owner):
+            return lax.dynamic_slice_in_dim(arr, lax.rem(owner + n_tp, n_tp) * loc_len, loc_len, axis=1)
+
+        def to_sequence(pieces):
+            out = jnp.zeros((n_rows, seq_len) + pieces[0].shape[2:], pieces[0].dtype)
+            for step, piece in enumerate(pieces):
+                out = lax.dynamic_update_slice_in_dim(out, piece, lax.rem(rank - step + n_tp, n_tp) * loc_len, axis=1)
+            return out
+
         resid_f32 = resid_loc.astype(jnp.float32)
         inv_rms = lax.rsqrt(jnp.mean(resid_f32 * resid_f32, axis=-1, keepdims=True) + EPS)
         normed = (resid_f32 * inv_rms * norm_gain).astype(jnp.bfloat16)
 
-        wqkv_full = lax.all_gather(wqkv_loc, "fsdp", axis=0, tiled=True)
-        wout_full = lax.all_gather(wout_loc, "fsdp", axis=0, tiled=True)
-        normed_all = lax.all_gather(normed, "tp", axis=1, tiled=True)
-        seq_len = normed_all.shape[1]
-        head_dim = wout_full.shape[0] // heads_loc
-        kv_loc = (wqkv_full.shape[1] // head_dim - heads_loc) // 2
-
-        qkv_proj = (jnp.dot(normed_all, wqkv_full, preferred_element_type=jnp.float32) + bqkv_loc.astype(jnp.float32)).astype(jnp.bfloat16)
+        wqkv_own = lax.all_gather(wqkv_loc, "fsdp", axis=0, tiled=True)
+        wout_ring = ring_gather(wout_loc, n_tp)
+        wout_all = lax.all_gather(jnp.concatenate(wout_ring, axis=0), "fsdp", axis=0, tiled=True)
+
+        def project(piece):
+            return (jnp.dot(piece, wqkv_own, preferred_element_type=jnp.float32) + bqkv_loc.astype(jnp.float32)).astype(jnp.bfloat16)
+
+        d_attn_rows = jnp.einsum("ntk,hk->nth", grad_loc, wout_all, preferred_element_type=jnp.float32).astype(jnp.bfloat16)
+        d_attn_rows = d_attn_rows.reshape(n_rows, loc_len, n_fsdp, n_tp, -1)
+        d_attn_send = [d_attn_rows[:, :, :, (n_tp - step) % n_tp].reshape(n_rows, loc_len, out_loc) for step in range(n_tp)]
+
+        normed_ring, qkv_pieces = [normed], [project(normed)]
+        held = ordered(normed, wout_ring[-1])
+        for step in range(1, n_tp):
+            held = tp_shift(held, 1, n_tp)
+            normed_ring.append(held)
+            qkv_pieces.append(project(held))
+            held = ordered(held, qkv_pieces[step - 1])
+
+        wqkv_ring = [wqkv_loc]
+        held = ordered(wqkv_loc, normed_ring[-1])
+        for _ in range(1, n_tp):
+            held = tp_shift(held, 1, n_tp)
+            wqkv_ring.append(held)
+            held = ordered(held, d_attn_send)
+        wqkv_rest = lax.all_gather(jnp.concatenate(wqkv_ring[1:], axis=1), "fsdp", axis=0, tiled=True)
+
+        qkv_proj = to_sequence(qkv_pieces)
         positions = jnp.arange(seq_len)
         queries, keys_rot, values = split_qkv(qkv_proj, positions, kv_loc, head_dim)
         pad_zeros = jnp.zeros((n_rows, WINDOW, kv_loc, head_dim), jnp.bfloat16)
         keys_ext = jnp.concatenate([pad_zeros, keys_rot], axis=1)
         values_ext = jnp.concatenate([pad_zeros, values], axis=1)
         attn_out, log_norm = attend_forward(queries, keys_ext, values_ext, sink_loc, 0)
-        attn_flat = attn_out.reshape(n_rows, seq_len, heads_loc * head_dim)
-        part_sum = jnp.dot(attn_flat, wout_full, preferred_element_type=jnp.float32)
-        proj_out = lax.psum_scatter(part_sum, "tp", scatter_dimension=1, tiled=True)
-        resid_out = (resid_f32 + proj_out + b_out.astype(jnp.float32)).astype(jnp.bfloat16)
-
-        grad_bout = lax.psum(jnp.sum(grad_loc, axis=(0, 1), dtype=jnp.float32), ("fsdp", "tp"))
-        grad_all = lax.all_gather(grad_loc, "tp", axis=1, tiled=True)
-        wout_part = jnp.einsum("nth,ntk->hk", attn_flat, grad_all, preferred_element_type=jnp.float32)
-        grad_wout = lax.psum_scatter(wout_part, "fsdp", scatter_dimension=0, tiled=True)
-        d_attn = jnp.einsum("ntk,hk->nth", grad_all, wout_full, preferred_element_type=jnp.float32).astype(jnp.bfloat16)
+        d_attn_send = ordered(d_attn_send, wqkv_ring[-1], attn_out)
+        d_attn_mine = exchange(d_attn_send, n_tp)
+        attn_flat = attn_out.reshape(n_rows, seq_len, out_loc)
+
+        d_attn = to_sequence(d_attn_mine)
+        bout_part = jnp.sum(grad_loc, axis=(0, 1), dtype=jnp.float32)
+        grad_hop = tp_shift(ordered(grad_loc, d_attn_mine, attn_out), 1, n_tp)
+        attn_mine = exchange(ordered([chunk_of(attn_flat, rank + step) for step in range(n_tp)], d_attn_mine), n_tp)
+        attn_rows = jnp.stack([piece.reshape(n_rows, loc_len, n_fsdp, -1) for piece in attn_mine], axis=3).reshape(n_rows, loc_len, n_tp * out_loc)
         dq_rot, dk_ext, dv_ext, sink_part = attend_backward(queries, keys_ext, values_ext, sink_loc, 0, log_norm, d_attn.reshape(attn_out.shape))
         cos_tab, sin_tab = rope_tables(positions, head_dim)
         d_query = rope_back(dq_rot.astype(jnp.float32), cos_tab[:, None, None], sin_tab[:, None, None]).astype(jnp.bfloat16)
         d_key = rope_back(dk_ext[:, WINDOW:].astype(jnp.bfloat16).astype(jnp.float32), cos_tab[:, None], sin_tab[:, None]).astype(jnp.bfloat16)
         d_value = dv_ext[:, WINDOW:].astype(jnp.bfloat16)
         d_qkv = jnp.concatenate([d_query, d_key[:, :, :, None], d_value[:, :, :, None]], axis=3).reshape(qkv_proj.shape)
-        wqkv_part = jnp.einsum("ntd,ntc->dc", normed_all, d_qkv, preferred_element_type=jnp.float32)
+
+        d_ring = jnp.concatenate([chunk_of(d_qkv, rank - step) for step in range(n_tp)], axis=1)
+        wqkv_part = jnp.einsum("ntd,ntc->dc", jnp.concatenate(normed_ring, axis=1), d_ring, preferred_element_type=jnp.float32)
         grad_wqkv = lax.psum_scatter(wqkv_part, "fsdp", scatter_dimension=0, tiled=True)
+        grad_ring = [grad_loc, grad_hop]
+        held = ordered(grad_hop, wqkv_part, attn_mine)
+        for _ in range(n_tp - 2):
+            held = tp_shift(held, 1, n_tp)
+            grad_ring.append(held)
+        attn_ring = jnp.concatenate([chunk_of(attn_flat, rank - step) for step in range(n_tp)], axis=1)
+        wout_part = jnp.einsum("nth,ntk->hk", attn_ring, jnp.concatenate(grad_ring, axis=1), preferred_element_type=jnp.float32)
+        grad_wout = lax.psum_scatter(wout_part, "fsdp", scatter_dimension=0, tiled=True)
+        d_mine = exchange(ordered([chunk_of(d_qkv, rank + step) for step in range(n_tp)], grad_ring[-1]), n_tp)
+        proj_out = jnp.dot(attn_rows, wout_all, preferred_element_type=jnp.float32)
+        resid_out = (resid_f32 + proj_out + b_out.astype(jnp.float32)).astype(jnp.bfloat16)
         grad_bqkv = lax.psum(jnp.sum(d_qkv, axis=(0, 1), dtype=jnp.float32), "fsdp")
         grad_sinks = lax.psum(sink_part, "fsdp")
-        normed_part = jnp.einsum("ntc,dc->ntd", d_qkv, wqkv_full, preferred_element_type=jnp.float32)
-        d_normed = lax.psum_scatter(normed_part, "tp", scatter_dimension=1, tiled=True)
+        d_normed = jnp.einsum("ntc,dc->ntd", d_mine[0], wqkv_own, preferred_element_type=jnp.float32) + jnp.einsum("ntc,dc->ntd", jnp.concatenate(d_mine[1:], axis=2), wqkv_rest, preferred_element_type=jnp.float32)
         grad_resid, gain_part = norm_backward(d_normed, resid_f32, inv_rms, norm_gain, grad_loc)
-        grad_gain = lax.psum(gain_part, ("fsdp", "tp"))
+        grad_gain, grad_bout = lax.psum((gain_part, bout_part), ("fsdp", "tp"))
         return (resid_out, grad_resid, grad_gain, grad_wqkv, grad_bqkv, grad_sinks, grad_wout, grad_bout)
 
     return jax.shard_map(device_step, mesh=mesh, in_specs=in_specs, out_specs=out_specs, check_vma=False)

time: 2420 us -> 1540 us (0.64)
  waiting for transfers between devices: 1930 us -> 910 us
  starting transfers between devices: 0.32 us -> 55.2 us
  matrix products: 323 us -> 375 us
  local copies, waits for them, and re-layouts: 30.5 us -> 61.3 us
    reduce_scatter x2 -> x0, waiting for transfers between devices: 917 us -> none  [the longest x1 513 us: device_step(): proj_out = lax.psum_scatter(part_sum, 'tp', scatter_dimension=1, tiled=True)]
    ppermute x0 -> x21, waiting for transfers between devices: none -> 768 us  [tp_shift(): lax.ppermute(value, 'tp', [(rank, (rank + step) % n_ranks) for rank in ra...]
    all_gather x4 -> x3, waiting for transfers between devices: 679 us -> 0.04 us  [the longest x1 0.02 us: device_step(): wqkv_own = lax.all_gather(wqkv_loc, 'fsdp', axis=0, tiled=True)]
    reduce_scatter x1, waiting for transfers between devices: 111 us -> 0.01 us  [device_step(): lax.psum_scatter(wout_part, 'fsdp', scatter_dimension=0, tiled=True)]
    reduce_scatter x1, waiting for transfers between devices: 223 us -> 140 us  [device_step(): lax.psum_scatter(wqkv_part, 'fsdp', scatter_dimension=0, tiled=True)]
    ppermute x0 -> x21, starting transfers between devices: none -> 55 us  [tp_shift(): lax.ppermute(value, 'tp', [(rank, (rank + step) % n_ranks) for rank in ra...]
    dot_general x6 -> x10, matrix products: 193 us -> 235 us  [the longest x4 56.1 us: project(): jnp.dot(piece, wqkv_own, preferred_element_type=jnp.float32)]
  transfers between devices with their start and end apart: 8 -> 26, of which waited for: 8 -> 16; matrix products, arithmetic and copies ran while one was open for 6% -> 32% of each run, Pallas kernels for 0% -> 0%
where the time goes in v1:
time: 1540 us
  waiting for transfers between devices  910 us (59%)
  matrix products  375 us (24%)
  other arithmetic  62.1 us (4%)
  local copies, waits for them, and re-layouts  61.3 us (4%)
  blocking collectives  55.9 us (4%)
  starting transfers between devices  55.2 us (4%)
    ppermute x21, waiting for transfers between devices, tp_shift(): lax.ppermute(value, 'tp', [(rank, (rank + step) % n_ranks) for rank in ra...  768 us
    reduce_scatter x1, waiting for transfers between devices, device_step(): lax.psum_scatter(wqkv_part, 'fsdp', scatter_dimension=0, tiled=True)  140 us
    dot_general x4, matrix products, project(): jnp.dot(piece, wqkv_own, preferred_element_type=jnp.float32)  56.1 us
    ppermute x21, starting transfers between devices, tp_shift(): lax.ppermute(value, 'tp', [(rank, (rank + step) % n_ranks) for rank in ra...  55 us
    psum x1, blocking collectives, device_step(): grad_gain, grad_bout = lax.psum((gain_part, bout_part), ('fsdp', 'tp'))  43 us
    dot_general x1, matrix products, device_step(): jnp.einsum('ntd,ntc->dc', jnp.concatenate(normed_ring, axis=1), d_ring, p...  36.2 us
    dot_general x24, matrix products, block_scores(): jnp.einsum('niegd,njed->negij', q_blk, k_blk, preferred_element_type=jnp....  34.7 us
    dot_general x1, matrix products, device_step(): jnp.einsum('ntk,hk->nth', grad_loc, wout_all, preferred_element_type=jnp....  33.1 us
  transfers between devices with their start and end apart: 26, of which 16 were waited for; matrix products, arithmetic and copies ran while one was open for 32% of the time, Pallas kernels for 0%

profile of v1, /device:TPU:0, one launch (start us, length us, event | category | flops | bytes accessed | tf_op | source)
XLA Modules:
  0.0 1535.1 jit_solution(1991362243728134990)
XLA Ops:
  7.9 3.1 collective-permute-start
  11.1 38.0 %collective-permute-done = bf16[160,5120]{1,0:T(8,128)(2,1)S(1)} collective-permute-done((bf16[160,5120]{1,0:T(8,128)(2,1)}, bf16[160,5120]{1,0:T(8,128)(2,1)S(1)}, u32[]{:S(2)}, u32[]{:S(2)}) %collective-permute-start) | collective-permute-done | bytes 1638432 | tf_op jit(solution)/shard_map/ppermute | solution.py:124
  49.1 38.8 %collective-permute-done.1 = bf16[160,5120]{1,0:T(8,128)(2,1)S(1)} collective-permute-done((bf16[160,5120]{1,0:T(8,128)(2,1)S(1)}, bf16[160,5120]{1,0:T(8,128)(2,1)S(1)}, u32[]{:S(2)}, u32[]{:S(2)}) %collective-permute-start.1) | collective-permute-done | bytes 1638432 | tf_op jit(solution)/shard_map/ppermute | solution.py:124
  87.9 37.9 %collective-permute-done.2 = bf16[160,5120]{1,0:T(8,128)(2,1)S(1)} collective-permute-done((bf16[160,5120]{1,0:T(8,128)(2,1)S(1)}, bf16[160,5120]{1,0:T(8,128)(2,1)S(1)}, u32[]{:S(2)}, u32[]{:S(2)}) %collective-permute-start.2) | collective-permute-done | bytes 1638432 | tf_op jit(solution)/shard_map/ppermute | solution.py:124
  125.8 4.7 pad_maximum_fusion.3
  130.6 3.1 fusion.83
  133.9 4.1 fusion.77
  138.0 17.0 %fusion.139 = bf16[1,384,1792]{2,1,0:T(8,128)(2,1)} fusion(bf16[5120,1792]{1,0:T(8,128)(2,1)} %all-gather.4.cloned.1.call-done, bf16[1,384,5120]{2,1,0:T(8,128)(2,1)} %fusion.77, f32[1792]{0:T(1024)S(1)} %convert_element_type.322), kind=kOutput, calls=%fused_computation.178 | convolution fusion | flops 7047806976 | bytes 23665664 | tf_op jit(solution)/shard_map/dot_general | solution.py:178
  155.0 68.6 %collective-permute-done.3 = bf16[1,384,5120]{2,1,0:T(8,128)(2,1)} collective-permute-done((bf16[1,384,5120]{2,1,0:T(8,128)(2,1)}, bf16[1,384,5120]{2,1,0:T(8,128)(2,1)}, u32[]{:S(2)}, u32[]{:S(2)}) %collective-permute-start.3) | collective-permute-done | bytes 3932192 | tf_op jit(solution)/shard_map/ppermute | solution.py:124
  223.6 10.7 fusion.142
  234.3 74.7 %collective-permute-done.4 = bf16[1,384,5120]{2,1,0:T(8,128)(2,1)S(1)} collective-permute-done((bf16[1,384,5120]{2,1,0:T(8,128)(2,1)}, bf16[1,384,5120]{2,1,0:T(8,128)(2,1)S(1)}, u32[]{:S(2)}, u32[]{:S(2)}) %collective-permute-start.4) | collective-permute-done | bytes 3932192 | tf_op jit(solution)/shard_map/ppermute | solution.py:124
  310.9 82.7 %collective-permute-done.5 = bf16[1,384,5120]{2,1,0:T(8,128)(2,1)} collective-permute-done((bf16[1,384,5120]{2,1,0:T(8,128)(2,1)S(1)}, bf16[1,384,5120]{2,1,0:T(8,128)(2,1)}, u32[]{:S(2)}, u32[]{:S(2)}) %collective-permute-start.5) | collective-permute-done | bytes 3932192 | tf_op jit(solution)/shard_map/ppermute | solution.py:124
  393.9 33.1 %convolution_convert_fusion.2 = bf16[5120,384]{1,0:T(8,128)(2,1)S(1)} fusion(bf16[5120,5120]{1,0:T(8,128)(2,1)} %all-gather.6.cloned.1.call-done, bf16[1,384,5120]{2,1,0:T(8,128)(2,1)} %param.13), kind=kOutput, calls=%fused_computation.130 | convolution fusion | flops 20134625280 | bytes 60293120 | tf_op jit(solution)/shard_map/ntk,hk->nth/dot_general | solution.py:180
  429.1 15.0 collective-permute-done.6
  444.1 50.0 %collective-permute-done.7 = bf16[640,1792]{1,0:T(8,128)(2,1)S(1)} collective-permute-done((bf16[640,1792]{1,0:T(8,128)(2,1)S(1)}, bf16[640,1792]{1,0:T(8,128)(2,1)S(1)}, u32[]{:S(2)}, u32[]{:S(2)}) %collective-permute-start.7) | collective-permute-done | bytes 2293792 | tf_op jit(solution)/shard_map/ppermute | solution.py:124
  494.1 46.0 %collective-permute-done.8 = bf16[640,1792]{1,0:T(8,128)(2,1)S(1)} collective-permute-done((bf16[640,1792]{1,0:T(8,128)(2,1)S(1)}, bf16[640,1792]{1,0:T(8,128)(2,1)S(1)}, u32[]{:S(2)}, u32[]{:S(2)}) %collective-permute-start.8) | collective-permute-done | bytes 2293792 | tf_op jit(solution)/shard_map/ppermute | solution.py:124
  540.0 3.1 pad_maximum_fusion.2
  549.5 3.8 broadcast_in_dim.94
  557.0 14.3 fusion.145
  574.5 14.1 fusion.148
  594.0 3.2 slice_convert_fusion
  600.7 6.5 copy.42
  608.2 2.3 broadcast.347.clone
  610.5 47.9 %while.39 = (s32[]{:T(128)}, bf16[1,1536,2,5,128]{1,4,3,2,0:T(8,128)(2,1)}, f32[1,2,5,1536]{3,2,1,0:T(8,128)S(1)}, bf16[1,1664,2,128]{1,3,2,0:T(8,128)(2,1)}, bf...) while((s32[]{:T(128)}, ...), condition=%wide.region_4.5_spmd, body=%wide.region_1.4_spmd.sunk | while | flops 170696832 | bytes 4993856 | solution.py:75
  658.9 3.4 collective-permute-start.11
  662.3 6.0 constant_dynamic-slice_fusion.2
  669.7 15.5 %collective-permute-done.9 = bf16[1,384,1280]{1,2,0:T(8,128)(2,1)} collective-permute-done((bf16[1,384,1280]{1,2,0:T(8,128)(2,1)}, bf16[1,384,1280]{1,2,0:T(8,128)(2,1)}, u32[]{:S(2)}, u32[]{:S(2)}) %collective-permute-start.9) | collective-permute-done | bytes 983072 | tf_op jit(solution)/shard_map/ppermute | solution.py:124
  685.3 32.2 %collective-permute-done.10 = bf16[1,384,1280]{1,2,0:T(8,128)(2,1)} collective-permute-done((bf16[1,384,1280]{1,2,0:T(8,128)(2,1)}, bf16[1,384,1280]{1,2,0:T(8,128)(2,1)}, u32[]{:S(2)}, u32[]{:S(2)}) %collective-permute-start.10) | collective-permute-done | bytes 983072 | tf_op jit(solution)/shard_map/ppermute | solution.py:124
  717.5 41.6 %collective-permute-start.14 = (bf16[1,384,1280]{1,2,0:T(8,128)(2,1)}, bf16[1,384,1280]{1,2,0:T(8,128)(2,1)}, u32[]{:S(2)}, u32[]{:S(2)}) collective-permute-start(bf16[1,384,1280]{1,2,0:T(8,128)(2,1)} %get-tuple-element.486), channel_id=1, source_target_pairs={{0,24},{8,0},{16,8},{24,16},{1,25},{9,1},{17,9},{25,17},{2,26},{10... | collective-permute-start | bytes 2949128 | tf_op jit(solution)/shard_map/ppermute | solution.py:124
  763.8 2.5 broadcast.347
  768.9 106.2 %while.40 = (s32[]{:T(128)}, bf16[1,1536,2,5,128]{1,4,3,2,0:T(8,128)(2,1)}, f32[1,1664,2,128]{1,3,2,0:T(8,128)}, f32[1,1664,2,128]{1,3,2,0:T(8,128)}, f32[2,5]{1...) while((s32[]{:T(128)}, ...), condition=%wide.region_8.0_spmd.clone, body=%wide.region_5.8_spmd.clone.sunk | while | flops 424021152 | bytes 11051006 | solution.py:106
  875.1 3.2 convert_element_type.341
  878.3 3.1 collective-permute-start.15
  888.1 3.9 constant_dynamic-slice_fusion.5
  892.0 36.2 %fusion.61 = f32[5120,1792]{1,0:T(8,128)} fusion(bf16[1,384,5120]{2,1,0:T(8,128)(2,1)} %collective-permute-done.5, bf16[1,384,5120]{2,1,0:T(8,128)(2,1)} %copy-done.23, bf16[1,384,5120]{2,1,0:T(8,128)(2,1)} %collective-permute-done.3, bf16[1,384,5120]{2,1,0:T(8,128)(2,1)} %fusion.77, bf16[1,384,1792]{1,2,0:T(8,128)(2,1)} %get-tuple-element.621, ...), kind=kOutput, calls=%fused_computation.88 | convolution fusion | flops 28270657536 | bytes 57933824 | tf_op jit(solution)/shard_map/ntd,ntc->dc/dot_general | solution.py:224
  928.3 35.2 %collective-permute-done.15 = bf16[1,384,5120]{2,1,0:T(8,128)(2,1)} collective-permute-done((bf16[1,384,5120]{2,1,0:T(8,128)(2,1)}, bf16[1,384,5120]{2,1,0:T(8,128)(2,1)}, u32[]{:S(2)}, u32[]{:S(2)}) %collective-permute-start.15) | collective-permute-done | bytes 3932192 | tf_op jit(solution)/shard_map/ppermute | solution.py:124
  963.5 83.4 %collective-permute-done.16 = bf16[1,384,5120]{2,1,0:T(8,128)(2,1)S(1)} collective-permute-done((bf16[1,384,5120]{2,1,0:T(8,128)(2,1)}, bf16[1,384,5120]{2,1,0:T(8,128)(2,1)S(1)}, u32[]{:S(2)}, u32[]{:S(2)}) %collective-permute-start.16) | collective-permute-done | bytes 3932192 | tf_op jit(solution)/shard_map/ppermute | solution.py:124
  1048.8 65.8 %collective-permute-done.17 = bf16[1,384,5120]{2,1,0:T(8,128)(2,1)S(1)} collective-permute-done((bf16[1,384,5120]{2,1,0:T(8,128)(2,1)S(1)}, bf16[1,384,5120]{2,1,0:T(8,128)(2,1)S(1)}, u32[]{:S(2)}, u32[]{:S(2)}) %collective-permute-start.17) | collective-permute-done | bytes 3932192 | tf_op jit(solution)/shard_map/ppermute | solution.py:124
  1116.5 27.3 %fusion.68 = f32[1280,5120]{1,0:T(8,128)} fusion(bf16[1,384,5120]{2,1,0:T(8,128)(2,1)} %copy-done.26, bf16[1,384,5120]{2,1,0:T(8,128)(2,1)} %copy-done.25, bf16[1,384,5120]{2,1,0:T(8,128)(2,1)} %collective-permute-done.15, bf16[1,384,5120]{2,1,0:T(8,128)(2,1)} %param.13, bf16[1,384,1280]{1,2,0:T(8,128)(2,1)} %get-tuple-element.630, ...), kind=kOutput, calls=%fused_computation.96 | convolution fusion | flops 20211302400 | bytes 45875200 | tf_op jit(solution)/shard_map/nth,ntk->hk/dot_general | solution.py:232
  1149.1 13.0 all-reduce.3
  1162.1 3.1 pad_maximum_fusion.5
  1168.6 30.9 %fusion.85 = bf16[1,384,5120]{2,1,0:T(8,128)(2,1)} fusion(bf16[1,384,5120]{2,1,0:T(8,128)(2,1)S(1)} %copy-done.1, bf16[384,5120]{0,1:T(8,128)(2,1)S(1)} %bitcast.350, bf16[5120,5120]{1,0:T(8,128)(2,1)} %all-gather.6.cloned.1.call-done, f32[5120]{0:T(1024)S(1)} %copy-done.18), kind=kOutput, calls=%fused_computation.123 | convolution fusion | flops 20140523520 | bytes 64245760 | tf_op jit(solution)/shard_map/dot_general | solution.py:235
  1199.5 84.3 %collective-permute-done.19 = bf16[1,384,1792]{1,2,0:T(8,128)(2,1)} collective-permute-done((bf16[1,384,1792]{1,2,0:T(8,128)(2,1)S(1)}, bf16[1,384,1792]{1,2,0:T(8,128)(2,1)}, u32[]{:S(2)}, u32[]{:S(2)}) %collective-permute-start.19) | collective-permute-done | bytes 1376288 | tf_op jit(solution)/shard_map/ppermute | solution.py:124
  1283.9 29.7 %fusion.95 = f32[384,5120]{1,0:T(8,128)} fusion(bf16[5120,5376]{1,0:T(8,128)(2,1)} %all-gather.8.cloned.1.call-done, bf16[1,384,1792]{1,2,0:T(8,128)(2,1)} %copy-done.27, bf16[1,384,1792]{1,2,0:T(8,128)(2,1)} %collective-permute-done.19, bf16[1,384,1792]{1,2,0:T(8,128)(2,1)} %collective-permute-done.18), kind=kOutput, calls=%fused_computation.141 | convolution fusion | flops 21151678464 | bytes 67043328 | tf_op jit(solution)/shard_map/ntc,dc->ntd/dot_general | solution.py:239
  1313.6 21.6 %fusion.88 = (f32[5120]{0:T(1024)S(1)}, f32[384]{0:T(512)S(1)}, bf16[384,5120]{1,0:T(8,128)(2,1)}) fusion(bf16[1,384,5120]{2,1,0:T(8,128)(2,1)} %param.12, f32[384]{0:T(512)S(1)} %copy-done.20, f32[5120]{0:T(1024)S(1)} %copy-done.17, f32[384,5120]{1,0:T(8,128)} %fusion.95, bf16[5120,1792]{1,0:T(8,128)(2,1)} %all-gather.4.cloned.1.call-done, ...), kind=kOutput, calls=%fused_computation.126 | convolution fusion | flops 7066085888 | bytes 35499008 | tf_op jit(solution)/shard_map/ntc,dc->ntd/dot_general | solution.py:239
  1335.2 9.9 convert_reduce_fusion.1
  1345.1 43.0 %all-reduce.2 = (f32[5120]{0:T(1024)}, f32[5120]{0:T(1024)}) all-reduce(f32[5120]{0:T(1024)S(1)} %get-tuple-element.570, f32[5120]{0:T(1024)S(1)} %get-tuple-element.636), channel_id=1, replica_groups=mesh['tp'=4,'fsdp'=8] {'fsdp','tp'}, use_global_device_ids=true, to_apply=%region_11.12 | all-reduce | flops 10240 | bytes 81920 | tf_op jit(solution)/shard_map/psum | solution.py:241
  1388.1 140.3 %reduce-scatter.3.cloned.1.call-done = f32[640,1792]{1,0:T(8,128)} async-done(((f32[5120,1792]{1,0:T(8,128)}), f32[640,1792]{1,0:T(8,128)}) %reduce-scatter.3.cloned.1.call-update) | async-done | bytes 4587536 | tf_op jit(solution)/shard_map/reduce_scatter | solution.py:225
  (392 shorter events, 209.4 us)
Async XLA Ops:
  7.2 130.8 %all-gather.4.cloned.1.call-start = ((), (), s32[]{:S(2)}) async-start(), calls=%async_computation.2 | async-start | bytes 20643840 | tf_op jit(solution)/shard_map/all_gather | solution.py:173
  7.9 386.0 %all-gather.6.cloned.1.call-start = ((), (), s32[]{:S(2)}) async-start(), calls=%async_computation.3 | async-start | bytes 58982400 | tf_op jit(solution)/shard_map/all_gather | solution.py:175
  7.9 41.1 %collective-permute-start = (bf16[160,5120]{1,0:T(8,128)(2,1)}, bf16[160,5120]{1,0:T(8,128)(2,1)S(1)}, u32[]{:S(2)}, u32[]{:S(2)}) collective-permute-start(bf16[160,5120]{1,0:T(8,128)(2,1)} %param.18), channel_id=1, source_target_pairs={{0,8},{8,16},{16,24},{24,0},{1,9},{9,17},{17,25},{25,1},{2,10},{10... | collective-permute-start | bytes 4915208 | tf_op jit(solution)/shard_map/ppermute | solution.py:124
  49.1 38.8 %collective-permute-start.1 = (bf16[160,5120]{1,0:T(8,128)(2,1)S(1)}, bf16[160,5120]{1,0:T(8,128)(2,1)S(1)}, u32[]{:S(2)}, u32[]{:S(2)}) collective-permute-start(bf16[160,5120]{1,0:T(8,128)(2,1)S(1)} %collective-permute-done), channel_id=1, source_target_pairs={{0,8},{8,16},{16,24},{24,0},{1,9},{9,17},{17,25},{25,1},{2,10},{10... | collective-permute-start | bytes 4915208 | tf_op jit(solution)/shard_map/ppermute | solution.py:124
  87.8 37.9 %collective-permute-start.2 = (bf16[160,5120]{1,0:T(8,128)(2,1)S(1)}, bf16[160,5120]{1,0:T(8,128)(2,1)S(1)}, u32[]{:S(2)}, u32[]{:S(2)}) collective-permute-start(bf16[160,5120]{1,0:T(8,128)(2,1)S(1)} %collective-permute-done.1), channel_id=1, source_target_pairs={{0,8},{8,16},{16,24},{24,0},{1,9},{9,17},{17,25},{25,1},{2,10},{10... | collective-permute-start | bytes 4915208 | tf_op jit(solution)/shard_map/ppermute | solution.py:124
  130.5 3.2 copy-start.16
  130.5 1153.3 %all-gather.8.cloned.1.call-start = ((), (), s32[]{:S(2)}) async-start(), calls=%async_computation.4 | async-start | bytes 61931520 | tf_op jit(solution)/shard_map/all_gather | solution.py:198
  130.6 3.3 copy-start
  133.9 4.1 copy-start.19
  133.9 4.1 copy-start.21
  137.9 85.7 %collective-permute-start.3 = (bf16[1,384,5120]{2,1,0:T(8,128)(2,1)}, bf16[1,384,5120]{2,1,0:T(8,128)(2,1)}, u32[]{:S(2)}, u32[]{:S(2)}) collective-permute-start(bf16[1,384,5120]{2,1,0:T(8,128)(2,1)} %fusion.77), channel_id=1, source_target_pairs={{0,8},{8,16},{16,24},{24,0},{1,9},{9,17},{17,25},{25,1},{2,10},{10... | collective-permute-start | bytes 11796488 | tf_op jit(solution)/shard_map/ppermute | solution.py:124
  138.0 85.6 %copy-start.22 = (bf16[5120,1792]{1,0:T(8,128)(2,1)S(1)}, bf16[5120,1792]{1,0:T(8,128)(2,1)}, u32[]{:S(2)}) copy-start(bf16[5120,1792]{1,0:T(8,128)(2,1)} %all-gather.4.cloned.1.call-done) | copy-start | bytes 55050244
  223.6 85.3 %collective-permute-start.4 = (bf16[1,384,5120]{2,1,0:T(8,128)(2,1)}, bf16[1,384,5120]{2,1,0:T(8,128)(2,1)S(1)}, u32[]{:S(2)}, u32[]{:S(2)}) collective-permute-start(bf16[1,384,5120]{2,1,0:T(8,128)(2,1)} %collective-permute-done.3), channel_id=1, source_target_pairs={{0,8},{8,16},{16,24},{24,0},{1,9},{9,17},{17,25},{25,1},{2,10},{10... | collective-permute-start | bytes 11796488 | tf_op jit(solution)/shard_map/ppermute | solution.py:124
  308.9 1.9 copy-start.23
  308.9 84.6 %collective-permute-start.5 = (bf16[1,384,5120]{2,1,0:T(8,128)(2,1)S(1)}, bf16[1,384,5120]{2,1,0:T(8,128)(2,1)}, u32[]{:S(2)}, u32[]{:S(2)}) collective-permute-start(bf16[1,384,5120]{2,1,0:T(8,128)(2,1)S(1)} %collective-permute-done.4), channel_id=1, source_target_pairs={{0,8},{8,16},{16,24},{24,0},{1,9},{9,17},{17,25},{25,1},{2,10},{10... | collective-permute-start | bytes 11796488 | tf_op jit(solution)/shard_map/ppermute | solution.py:124
  393.6 50.5 %collective-permute-start.6 = (bf16[640,1792]{1,0:T(8,128)(2,1)}, bf16[640,1792]{1,0:T(8,128)(2,1)S(1)}, u32[]{:S(2)}, u32[]{:S(2)}) collective-permute-start(bf16[640,1792]{1,0:T(8,128)(2,1)} %param.15), channel_id=1, source_target_pairs={{0,8},{8,16},{16,24},{24,0},{1,9},{9,17},{17,25},{25,1},{2,10},{10... | collective-permute-start | bytes 6881288 | tf_op jit(solution)/shard_map/ppermute | solution.py:124
  444.1 50.0 %collective-permute-start.7 = (bf16[640,1792]{1,0:T(8,128)(2,1)S(1)}, bf16[640,1792]{1,0:T(8,128)(2,1)S(1)}, u32[]{:S(2)}, u32[]{:S(2)}) collective-permute-start(bf16[640,1792]{1,0:T(8,128)(2,1)S(1)} %collective-permute-done.6), channel_id=1, source_target_pairs={{0,8},{8,16},{16,24},{24,0},{1,9},{9,17},{17,25},{25,1},{2,10},{10... | collective-permute-start | bytes 6881288 | tf_op jit(solution)/shard_map/ppermute | solution.py:124
  494.1 46.0 %collective-permute-start.8 = (bf16[640,1792]{1,0:T(8,128)(2,1)S(1)}, bf16[640,1792]{1,0:T(8,128)(2,1)S(1)}, u32[]{:S(2)}, u32[]{:S(2)}) collective-permute-start(bf16[640,1792]{1,0:T(8,128)(2,1)S(1)} %collective-permute-done.7), channel_id=1, source_target_pairs={{0,8},{8,16},{16,24},{24,0},{1,9},{9,17},{17,25},{25,1},{2,10},{10... | collective-permute-start | bytes 6881288 | tf_op jit(solution)/shard_map/ppermute | solution.py:124
  543.2 2.2 copy-start.11
  543.2 844.9 %reduce-scatter.5.cloned.1.call-start = ((), (), s32[]{:S(2)}) async-start(), calls=%async_computation.6 | async-start | bytes 29491200 | tf_op jit(solution)/shard_map/reduce_scatter | solution.py:233
  549.5 3.8 copy-start.4
  553.3 3.7 copy-start.24
  658.4 26.9 %collective-permute-start.9 = (bf16[1,384,1280]{1,2,0:T(8,128)(2,1)}, bf16[1,384,1280]{1,2,0:T(8,128)(2,1)}, u32[]{:S(2)}, u32[]{:S(2)}) collective-permute-start(bf16[1,384,1280]{1,2,0:T(8,128)(2,1)} %bitcast.360), channel_id=1, source_target_pairs={{0,8},{8,16},{16,24},{24,0},{1,9},{9,17},{17,25},{25,1},{2,10},{10... | collective-permute-start | bytes 2949128 | tf_op jit(solution)/shard_map/ppermute | solution.py:124
  658.5 59.0 %collective-permute-start.10 = (bf16[1,384,1280]{1,2,0:T(8,128)(2,1)}, bf16[1,384,1280]{1,2,0:T(8,128)(2,1)}, u32[]{:S(2)}, u32[]{:S(2)}) collective-permute-start(bf16[1,384,1280]{1,2,0:T(8,128)(2,1)} %bitcast.359), channel_id=1, source_target_pairs={{0,16},{8,24},{16,0},{24,8},{1,17},{9,25},{17,1},{25,9},{2,18},{10... | collective-permute-start | bytes 2949128 | tf_op jit(solution)/shard_map/ppermute | solution.py:124
  658.9 58.6 %collective-permute-start.11 = (bf16[1,384,1280]{1,2,0:T(8,128)(2,1)}, bf16[1,384,1280]{1,2,0:T(8,128)(2,1)}, u32[]{:S(2)}, u32[]{:S(2)}) collective-permute-start(bf16[1,384,1280]{1,2,0:T(8,128)(2,1)} %bitcast.358), channel_id=1, source_target_pairs={{0,24},{8,0},{16,8},{24,16},{1,25},{9,1},{17,9},{25,17},{2,26},{10... | collective-permute-start | bytes 2949128 | tf_op jit(solution)/shard_map/ppermute | solution.py:124
  717.5 210.8 %collective-permute-start.14 = (bf16[1,384,1280]{1,2,0:T(8,128)(2,1)}, bf16[1,384,1280]{1,2,0:T(8,128)(2,1)}, u32[]{:S(2)}, u32[]{:S(2)}) collective-permute-start(bf16[1,384,1280]{1,2,0:T(8,128)(2,1)} %get-tuple-element.486), channel_id=1, source_target_pairs={{0,24},{8,0},{16,8},{24,16},{1,25},{9,1},{17,9},{25,17},{2,26},{10... | collective-permute-start | bytes 2949128 | tf_op jit(solution)/shard_map/ppermute | solution.py:124
  759.0 169.2 %collective-permute-start.13 = (bf16[1,384,1280]{1,2,0:T(8,128)(2,1)}, bf16[1,384,1280]{1,2,0:T(8,128)(2,1)}, u32[]{:S(2)}, u32[]{:S(2)}) collective-permute-start(bf16[1,384,1280]{1,2,0:T(8,128)(2,1)} %get-tuple-element.485), channel_id=1, source_target_pairs={{0,16},{8,24},{16,0},{24,8},{1,17},{9,25},{17,1},{25,9},{2,18},{10... | collective-permute-start | bytes 2949128 | tf_op jit(solution)/shard_map/ppermute | solution.py:124
  759.0 169.2 %collective-permute-start.12 = (bf16[1,384,1280]{1,2,0:T(8,128)(2,1)}, bf16[1,384,1280]{1,2,0:T(8,128)(2,1)}, u32[]{:S(2)}, u32[]{:S(2)}) collective-permute-start(bf16[1,384,1280]{1,2,0:T(8,128)(2,1)} %get-tuple-element.484), channel_id=1, source_target_pairs={{0,8},{8,16},{16,24},{24,0},{1,9},{9,17},{17,25},{25,1},{2,10},{10... | collective-permute-start | bytes 2949128 | tf_op jit(solution)/shard_map/ppermute | solution.py:124
  763.8 5.1 copy-start.3
  878.3 85.2 %collective-permute-start.15 = (bf16[1,384,5120]{2,1,0:T(8,128)(2,1)}, bf16[1,384,5120]{2,1,0:T(8,128)(2,1)}, u32[]{:S(2)}, u32[]{:S(2)}) collective-permute-start(bf16[1,384,5120]{2,1,0:T(8,128)(2,1)} %param.13), channel_id=1, source_target_pairs={{0,8},{8,16},{16,24},{24,0},{1,9},{9,17},{17,25},{25,1},{2,10},{10... | collective-permute-start | bytes 11796488 | tf_op jit(solution)/shard_map/ppermute | solution.py:124
  883.2 3.5 copy-start.9
  963.5 83.4 %collective-permute-start.16 = (bf16[1,384,5120]{2,1,0:T(8,128)(2,1)}, bf16[1,384,5120]{2,1,0:T(8,128)(2,1)S(1)}, u32[]{:S(2)}, u32[]{:S(2)}) collective-permute-start(bf16[1,384,5120]{2,1,0:T(8,128)(2,1)} %collective-permute-done.15), channel_id=1, source_target_pairs={{0,8},{8,16},{16,24},{24,0},{1,9},{9,17},{17,25},{25,1},{2,10},{10... | collective-permute-start | bytes 11796488 | tf_op jit(solution)/shard_map/ppermute | solution.py:124
  1048.8 65.8 %collective-permute-start.17 = (bf16[1,384,5120]{2,1,0:T(8,128)(2,1)S(1)}, bf16[1,384,5120]{2,1,0:T(8,128)(2,1)S(1)}, u32[]{:S(2)}, u32[]{:S(2)}) collective-permute-start(bf16[1,384,5120]{2,1,0:T(8,128)(2,1)S(1)} %collective-permute-done.16), channel_id=1, source_target_pairs={{0,8},{8,16},{16,24},{24,0},{1,9},{9,17},{17,25},{25,1},{2,10},{10... | collective-permute-start | bytes 11796488 | tf_op jit(solution)/shard_map/ppermute | solution.py:124
  1143.8 1.9 copy-start.8
  1143.8 384.6 %reduce-scatter.3.cloned.1.call-start = ((), (), s32[]{:S(2)}) async-start(), calls=%async_computation.5 | async-start | bytes 41287680 | tf_op jit(solution)/shard_map/reduce_scatter | solution.py:225
  1147.6 14.5 copy-start.6
  1147.6 17.6 %copy-start.15 = (bf16[1,384,1792]{1,2,0:T(8,128)(2,1)S(1)}, bf16[1,384,1792]{1,2,0:T(8,128)(2,1)}, u32[]{:S(2)}) copy-start(bf16[1,384,1792]{1,2,0:T(8,128)(2,1)} %get-tuple-element.496) | copy-start | bytes 4128772
  1162.1 4.8 copy-start.14
  1162.1 4.8 copy-start.13
  1162.1 6.5 copy-start.1
  1162.1 6.5 copy-start.18
  1165.2 34.3 %collective-permute-start.20 = (bf16[1,384,1792]{1,2,0:T(8,128)(2,1)S(1)}, bf16[1,384,1792]{1,2,0:T(8,128)(2,1)S(1)}, u32[]{:S(2)}, u32[]{:S(2)}) collective-permute-start(bf16[1,384,1792]{1,2,0:T(8,128)(2,1)S(1)} %copy-done.15), channel_id=1, source_target_pairs={{0,24},{8,0},{16,8},{24,16},{1,25},{9,1},{17,9},{25,17},{2,26},{10... | collective-permute-start | bytes 4128776 | tf_op jit(solution)/shard_map/ppermute | solution.py:124
  1166.9 116.9 %collective-permute-start.19 = (bf16[1,384,1792]{1,2,0:T(8,128)(2,1)S(1)}, bf16[1,384,1792]{1,2,0:T(8,128)(2,1)}, u32[]{:S(2)}, u32[]{:S(2)}) collective-permute-start(bf16[1,384,1792]{1,2,0:T(8,128)(2,1)S(1)} %copy-done.14), channel_id=1, source_target_pairs={{0,16},{8,24},{16,0},{24,8},{1,17},{9,25},{17,1},{25,9},{2,18},{10... | collective-permute-start | bytes 4128776 | tf_op jit(solution)/shard_map/ppermute | solution.py:124
  1166.9 116.9 %collective-permute-start.18 = (bf16[1,384,1792]{1,2,0:T(8,128)(2,1)S(1)}, bf16[1,384,1792]{1,2,0:T(8,128)(2,1)}, u32[]{:S(2)}, u32[]{:S(2)}) collective-permute-start(bf16[1,384,1792]{1,2,0:T(8,128)(2,1)S(1)} %copy-done.13), channel_id=1, source_target_pairs={{0,8},{8,16},{16,24},{24,0},{1,9},{9,17},{17,25},{25,1},{2,10},{10... | collective-permute-start | bytes 4128776 | tf_op jit(solution)/shard_map/ppermute | solution.py:124
  1199.5 114.1 %copy-start.12 = (bf16[1,384,1792]{1,2,0:T(8,128)(2,1)S(1)}, bf16[1,384,1792]{1,2,0:T(8,128)(2,1)}, u32[]{:S(2)}) copy-start(bf16[1,384,1792]{1,2,0:T(8,128)(2,1)} %get-tuple-element.493) | copy-start | bytes 4128772
  1199.5 114.1 %copy-start.17 = (f32[5120]{0:T(1024)S(1)}, f32[5120]{0:T(1024)}, u32[]{:S(2)}) copy-start(f32[5120]{0:T(1024)} %param.14) | copy-start | bytes 61444
  1199.5 114.1 %copy-start.20 = (f32[384]{0:T(512)S(1)}, f32[384]{0:T(512)}, u32[]{:S(2)}) copy-start(f32[384]{0:T(512)} %copy-done.19) | copy-start | bytes 4612
  1199.5 84.3 %copy-start.27 = (bf16[1,384,1792]{1,2,0:T(8,128)(2,1)}, bf16[1,384,1792]{1,2,0:T(8,128)(2,1)S(1)}, u32[]{:S(2)}) copy-start(bf16[1,384,1792]{1,2,0:T(8,128)(2,1)S(1)} %collective-permute-done.20) | copy-start | bytes 4128772
  (7 other events, 9.8 us)
Sparse Core Ops, SparseCore 0:
  9.9 99.0 all-gather.3
  130.6 238.6 all-gather.5
  543.3 249.2 all-gather.7
  1143.9 159.4 reduce-scatter.4
  1307.5 220.7 reduce-scatter.2

commit v2 on v1

--- a/solution.py
+++ b/solution.py
@@ -173,30 +173,25 @@
         wqkv_own = lax.all_gather(wqkv_loc, "fsdp", axis=0, tiled=True)
         wout_ring = ring_gather(wout_loc, n_tp)
         wout_all = lax.all_gather(jnp.concatenate(wout_ring, axis=0), "fsdp", axis=0, tiled=True)
+        wqkv_ring = ring_gather(wqkv_loc, n_tp, wout_ring[-1])
+        wqkv_rest = lax.all_gather(jnp.concatenate(wqkv_ring[1:], axis=1), "fsdp", axis=0, tiled=True)
 
         def project(piece):
             return (jnp.dot(piece, wqkv_own, preferred_element_type=jnp.float32) + bqkv_loc.astype(jnp.float32)).astype(jnp.bfloat16)
 
-        d_attn_rows = jnp.einsum("ntk,hk->nth", grad_loc, wout_all, preferred_element_type=jnp.float32).astype(jnp.bfloat16)
-        d_attn_rows = d_attn_rows.reshape(n_rows, loc_len, n_fsdp, n_tp, -1)
+        d_attn_rows = jnp.einsum("ntk,hk->nth", grad_loc, wout_all, preferred_element_type=jnp.float32).astype(jnp.bfloat16).reshape(n_rows, loc_len, n_fsdp, n_tp, -1)
         d_attn_send = [d_attn_rows[:, :, :, (n_tp - step) % n_tp].reshape(n_rows, loc_len, out_loc) for step in range(n_tp)]
 
         normed_ring, qkv_pieces = [normed], [project(normed)]
-        held = ordered(normed, wout_ring[-1])
+        held = ordered(normed, wqkv_ring[-1])
         for step in range(1, n_tp):
             held = tp_shift(held, 1, n_tp)
             normed_ring.append(held)
             qkv_pieces.append(project(held))
-            held = ordered(held, qkv_pieces[step - 1])
-
-        wqkv_ring = [wqkv_loc]
-        held = ordered(wqkv_loc, normed_ring[-1])
-        for _ in range(1, n_tp):
-            held = tp_shift(held, 1, n_tp)
-            wqkv_ring.append(held)
-            held = ordered(held, d_attn_send)
-        wqkv_rest = lax.all_gather(jnp.concatenate(wqkv_ring[1:], axis=1), "fsdp", axis=0, tiled=True)
-
+            held = ordered(held, qkv_pieces[step - 1], d_attn_send) if step == n_tp - 2 else ordered(held, qkv_pieces[step - 1])
+
+        d_attn_send = ordered(d_attn_send, normed_ring[-1])
+        d_attn_mine = exchange(d_attn_send, n_tp)
         qkv_proj = to_sequence(qkv_pieces)
         positions = jnp.arange(seq_len)
         queries, keys_rot, values = split_qkv(qkv_proj, positions, kv_loc, head_dim)
@@ -204,8 +199,6 @@
         keys_ext = jnp.concatenate([pad_zeros, keys_rot], axis=1)
         values_ext = jnp.concatenate([pad_zeros, values], axis=1)
         attn_out, log_norm = attend_forward(queries, keys_ext, values_ext, sink_loc, 0)
-        d_attn_send = ordered(d_attn_send, wqkv_ring[-1], attn_out)
-        d_attn_mine = exchange(d_attn_send, n_tp)
         attn_flat = attn_out.reshape(n_rows, seq_len, out_loc)
 
         d_attn = to_sequence(d_attn_mine)
@@ -224,19 +217,20 @@
         wqkv_part = jnp.einsum("ntd,ntc->dc", jnp.concatenate(normed_ring, axis=1), d_ring, preferred_element_type=jnp.float32)
         grad_wqkv = lax.psum_scatter(wqkv_part, "fsdp", scatter_dimension=0, tiled=True)
         grad_ring = [grad_loc, grad_hop]
+        grad_bqkv, grad_sinks = lax.psum((jnp.sum(d_qkv, axis=(0, 1), dtype=jnp.float32), sink_part), "fsdp")
         held = ordered(grad_hop, wqkv_part, attn_mine)
-        for _ in range(n_tp - 2):
+        for _ in range(2, n_tp):
             held = tp_shift(held, 1, n_tp)
             grad_ring.append(held)
+            held = ordered(held, grad_bqkv, grad_sinks)
         attn_ring = jnp.concatenate([chunk_of(attn_flat, rank - step) for step in range(n_tp)], axis=1)
         wout_part = jnp.einsum("nth,ntk->hk", attn_ring, jnp.concatenate(grad_ring, axis=1), preferred_element_type=jnp.float32)
         grad_wout = lax.psum_scatter(wout_part, "fsdp", scatter_dimension=0, tiled=True)
-        d_mine = exchange(ordered([chunk_of(d_qkv, rank + step) for step in range(n_tp)], grad_ring[-1]), n_tp)
+        d_mine = exchange(ordered([chunk_of(d_qkv, rank + step) for step in range(n_tp)], wout_part), n_tp)
         proj_out = jnp.dot(attn_rows, wout_all, preferred_element_type=jnp.float32)
         resid_out = (resid_f32 + proj_out + b_out.astype(jnp.float32)).astype(jnp.bfloat16)
-        grad_bqkv = lax.psum(jnp.sum(d_qkv, axis=(0, 1), dtype=jnp.float32), "fsdp")
-        grad_sinks = lax.psum(sink_part, "fsdp")
-        d_normed = jnp.einsum("ntc,dc->ntd", d_mine[0], wqkv_own, preferred_element_type=jnp.float32) + jnp.einsum("ntc,dc->ntd", jnp.concatenate(d_mine[1:], axis=2), wqkv_rest, preferred_element_type=jnp.float32)
+        d_normed = jnp.einsum("ntc,dc->ntd", d_mine[0], wqkv_own, preferred_element_type=jnp.float32)
+        d_normed = d_normed + jnp.einsum("ntc,dc->ntd", jnp.concatenate(d_mine[1:], axis=2), wqkv_rest, preferred_element_type=jnp.float32)
         grad_resid, gain_part = norm_backward(d_normed, resid_f32, inv_rms, norm_gain, grad_loc)
         grad_gain, grad_bout = lax.psum((gain_part, bout_part), ("fsdp", "tp"))
         return (resid_out, grad_resid, grad_gain, grad_wqkv, grad_bqkv, grad_sinks, grad_wout, grad_bout)

time: 1540 us -> 1470 us (0.955)
  waiting for transfers between devices: 910 us -> 847 us
    ppermute x21, waiting for transfers between devices: 768 us -> 671 us  [tp_shift(): lax.ppermute(value, 'tp', [(rank, (rank + step) % n_ranks) for rank in ra...]
    reduce_scatter x1, waiting for transfers between devices: 140 us -> 175 us  [device_step(): lax.psum_scatter(wqkv_part, 'fsdp', scatter_dimension=0, tiled=True)]
  transfers between devices with their start and end apart: 26 -> 26, of which waited for: 16 -> 15; matrix products, arithmetic and copies ran while one was open for 32% -> 33% of each run, Pallas kernels for 0% -> 0%
where the time goes in v2:
time: 1470 us
  waiting for transfers between devices  847 us (58%)
  matrix products  382 us (26%)
  other arithmetic  56.7 us (4%)
  blocking collectives  55.7 us (4%)
  starting transfers between devices  55.3 us (4%)
  local copies, waits for them, and re-layouts  52.5 us (4%)
    ppermute x21, waiting for transfers between devices, tp_shift(): lax.ppermute(value, 'tp', [(rank, (rank + step) % n_ranks) for rank in ra...  671 us
    reduce_scatter x1, waiting for transfers between devices, device_step(): lax.psum_scatter(wqkv_part, 'fsdp', scatter_dimension=0, tiled=True)  175 us
    dot_general x4, matrix products, project(): jnp.dot(piece, wqkv_own, preferred_element_type=jnp.float32)  61.5 us
    ppermute x21, starting transfers between devices, tp_shift(): lax.ppermute(value, 'tp', [(rank, (rank + step) % n_ranks) for rank in ra...  55.1 us
    psum x1, blocking collectives, device_step(): grad_gain, grad_bout = lax.psum((gain_part, bout_part), ('fsdp', 'tp'))  42 us
    dot_general x1, matrix products, device_step(): proj_out = jnp.dot(attn_rows, wout_all, preferred_element_type=jnp.float32)  36.4 us
    dot_general x1, matrix products, device_step(): jnp.einsum('ntd,ntc->dc', jnp.concatenate(normed_ring, axis=1), d_ring, p...  36.3 us
    dot_general x1, matrix products, device_step(): jnp.einsum('ntc,dc->ntd', jnp.concatenate(d_mine[1:], axis=2), wqkv_rest,...  35.4 us
  transfers between devices with their start and end apart: 26, of which 15 were waited for; matrix products, arithmetic and copies ran while one was open for 33% of the time, Pallas kernels for 0%

profile of v2, /device:TPU:0, one launch (start us, length us, event | category | flops | bytes accessed | tf_op | source)
XLA Modules:
  0.0 1465.5 jit_solution(1389909929280933252)
XLA Ops:
  7.9 3.1 collective-permute-start
  11.1 38.0 %collective-permute-done = bf16[160,5120]{1,0:T(8,128)(2,1)S(1)} collective-permute-done((bf16[160,5120]{1,0:T(8,128)(2,1)}, bf16[160,5120]{1,0:T(8,128)(2,1)S(1)}, u32[]{:S(2)}, u32[]{:S(2)}) %collective-permute-start) | collective-permute-done | bytes 1638432 | tf_op jit(solution)/shard_map/ppermute | solution.py:124
  49.1 38.8 %collective-permute-done.1 = bf16[160,5120]{1,0:T(8,128)(2,1)S(1)} collective-permute-done((bf16[160,5120]{1,0:T(8,128)(2,1)S(1)}, bf16[160,5120]{1,0:T(8,128)(2,1)S(1)}, u32[]{:S(2)}, u32[]{:S(2)}) %collective-permute-start.1) | collective-permute-done | bytes 1638432 | tf_op jit(solution)/shard_map/ppermute | solution.py:124
  87.9 37.9 %collective-permute-done.2 = bf16[160,5120]{1,0:T(8,128)(2,1)S(1)} collective-permute-done((bf16[160,5120]{1,0:T(8,128)(2,1)S(1)}, bf16[160,5120]{1,0:T(8,128)(2,1)S(1)}, u32[]{:S(2)}, u32[]{:S(2)}) %collective-permute-start.2) | collective-permute-done | bytes 1638432 | tf_op jit(solution)/shard_map/ppermute | solution.py:124
  125.8 4.7 pad_maximum_fusion.3
  132.1 51.1 %collective-permute-done.3 = bf16[640,1792]{1,0:T(8,128)(2,1)S(1)} collective-permute-done((bf16[640,1792]{1,0:T(8,128)(2,1)S(1)}, bf16[640,1792]{1,0:T(8,128)(2,1)S(1)}, u32[]{:S(2)}, u32[]{:S(2)}) %collective-permute-start.3) | collective-permute-done | bytes 2293792 | tf_op jit(solution)/shard_map/ppermute | solution.py:124
  183.2 50.2 %collective-permute-done.4 = bf16[640,1792]{1,0:T(8,128)(2,1)S(1)} collective-permute-done((bf16[640,1792]{1,0:T(8,128)(2,1)S(1)}, bf16[640,1792]{1,0:T(8,128)(2,1)S(1)}, u32[]{:S(2)}, u32[]{:S(2)}) %collective-permute-start.4) | collective-permute-done | bytes 2293792 | tf_op jit(solution)/shard_map/ppermute | solution.py:124
  233.5 49.4 %collective-permute-done.5 = bf16[640,1792]{1,0:T(8,128)(2,1)S(1)} collective-permute-done((bf16[640,1792]{1,0:T(8,128)(2,1)S(1)}, bf16[640,1792]{1,0:T(8,128)(2,1)S(1)}, u32[]{:S(2)}, u32[]{:S(2)}) %collective-permute-start.5) | collective-permute-done | bytes 2293792 | tf_op jit(solution)/shard_map/ppermute | solution.py:124
  282.8 3.2 pad_maximum_fusion.2
  286.1 3.1 fusion.83
  289.4 3.2 fusion.77
  294.4 14.9 %fusion.138 = bf16[1,384,1792]{2,1,0:T(8,128)(2,1)} fusion(bf16[5120,1792]{1,0:T(8,128)(2,1)} %all-gather.4.cloned.1.call-done, bf16[1,384,5120]{2,1,0:T(8,128)(2,1)} %fusion.77, f32[1792]{0:T(1024)S(1)} %convert_element_type.322), kind=kOutput, calls=%fused_computation.177 | convolution fusion | flops 7047806976 | bytes 23665664 | tf_op jit(solution)/shard_map/dot_general | solution.py:180
  311.1 65.6 %collective-permute-done.6 = bf16[1,384,5120]{2,1,0:T(8,128)(2,1)} collective-permute-done((bf16[1,384,5120]{2,1,0:T(8,128)(2,1)}, bf16[1,384,5120]{2,1,0:T(8,128)(2,1)}, u32[]{:S(2)}, u32[]{:S(2)}) %collective-permute-start.6) | collective-permute-done | bytes 3932192 | tf_op jit(solution)/shard_map/ppermute | solution.py:124
  376.7 17.9 %fusion.141 = bf16[1,384,1792]{2,1,0:T(8,128)(2,1)} fusion(bf16[5120,1792]{1,0:T(8,128)(2,1)} %all-gather.4.cloned.1.call-done, bf16[1,384,5120]{2,1,0:T(8,128)(2,1)} %collective-permute-done.6, f32[1792]{0:T(1024)S(1)} %convert_element_type.322), kind=kOutput, calls=%fused_computation.178 | convolution fusion | flops 7047806976 | bytes 23665664 | tf_op jit(solution)/shard_map/dot_general | solution.py:180
  394.6 2.5 copy.37
  397.3 33.1 %convolution_convert_fusion.2 = bf16[5120,384]{1,0:T(8,128)(2,1)S(1)} fusion(bf16[5120,5120]{1,0:T(8,128)(2,1)} %all-gather.6.cloned.1.call-done, bf16[1,384,5120]{2,1,0:T(8,128)(2,1)} %param.13), kind=kOutput, calls=%fused_computation.130 | convolution fusion | flops 20134625280 | bytes 60293120 | tf_op jit(solution)/shard_map/ntk,hk->nth/dot_general | solution.py:182
  432.6 49.9 %collective-permute-done.7 = bf16[1,384,5120]{2,1,0:T(8,128)(2,1)} collective-permute-done((bf16[1,384,5120]{2,1,0:T(8,128)(2,1)}, bf16[1,384,5120]{2,1,0:T(8,128)(2,1)}, u32[]{:S(2)}, u32[]{:S(2)}) %collective-permute-start.7) | collective-permute-done | bytes 3932192 | tf_op jit(solution)/shard_map/ppermute | solution.py:124
  482.4 2.7 broadcast_in_dim.94
  487.7 14.4 fusion.144
  505.2 55.9 %collective-permute-done.8 = bf16[1,384,5120]{2,1,0:T(8,128)(2,1)} collective-permute-done((bf16[1,384,5120]{2,1,0:T(8,128)(2,1)}, bf16[1,384,5120]{2,1,0:T(8,128)(2,1)}, u32[]{:S(2)}, u32[]{:S(2)}) %collective-permute-start.8) | collective-permute-done | bytes 3932192 | tf_op jit(solution)/shard_map/ppermute | solution.py:124
  561.1 14.4 fusion.147
  580.9 3.5 slice_convert_fusion
  587.8 6.3 copy.42
  594.1 4.2 collective-permute-start.11
  599.3 2.3 broadcast.347.clone
  601.6 47.6 %while.39 = (s32[]{:T(128)}, bf16[1,1536,2,5,128]{1,4,3,2,0:T(8,128)(2,1)}, f32[1,2,5,1536]{3,2,1,0:T(8,128)S(1)}, bf16[1,1664,2,128]{1,3,2,0:T(8,128)(2,1)}, bf...) while((s32[]{:T(128)}, ...), condition=%wide.region_4.5_spmd, body=%wide.region_1.4_spmd.sunk | while | flops 170696832 | bytes 4993856 | solution.py:75
  651.6 3.0 constant_dynamic-slice_fusion.5
  654.6 40.9 %collective-permute-start.14 = (bf16[1,384,1280]{1,2,0:T(8,128)(2,1)}, bf16[1,384,1280]{1,2,0:T(8,128)(2,1)}, u32[]{:S(2)}, u32[]{:S(2)}) collective-permute-start(bf16[1,384,1280]{1,2,0:T(8,128)(2,1)} %get-tuple-element.483), channel_id=1, source_target_pairs={{0,24},{8,0},{16,8},{24,16},{1,25},{9,1},{17,9},{25,17},{2,26},{10... | collective-permute-start | bytes 2949128 | tf_op jit(solution)/shard_map/ppermute | solution.py:124
  700.3 2.5 broadcast.347
  705.4 106.1 %while.40 = (s32[]{:T(128)}, bf16[1,1536,2,5,128]{1,4,3,2,0:T(8,128)(2,1)}, f32[1,1664,2,128]{1,3,2,0:T(8,128)}, f32[1,1664,2,128]{1,3,2,0:T(8,128)}, f32[2,5]{1...) while((s32[]{:T(128)}, ...), condition=%wide.region_8.0_spmd.clone, body=%wide.region_5.8_spmd.clone.sunk | while | flops 424021152 | bytes 11051006 | solution.py:106
  811.5 3.2 convert_element_type.341
  814.7 3.1 collective-permute-start.15
  824.5 3.9 constant_dynamic-slice_fusion.2
  828.4 36.3 %fusion.61 = f32[5120,1792]{1,0:T(8,128)} fusion(bf16[1,384,5120]{2,1,0:T(8,128)(2,1)} %collective-permute-done.8, bf16[1,384,5120]{2,1,0:T(8,128)(2,1)} %collective-permute-done.7, bf16[1,384,5120]{2,1,0:T(8,128)(2,1)} %collective-permute-done.6, bf16[1,384,5120]{2,1,0:T(8,128)(2,1)} %fusion.77, bf16[1,384,1792]{1,2,0:T(8,128)(2,1)} %get-tuple-element.619, ...), kind=kOutput, calls=%fused_computation.88 | convolution fusion | flops 28270657536 | bytes 57933824 | tf_op jit(solution)/shard_map/ntd,ntc->dc/dot_general | solution.py:217
  864.7 35.3 %collective-permute-done.15 = bf16[1,384,5120]{2,1,0:T(8,128)(2,1)} collective-permute-done((bf16[1,384,5120]{2,1,0:T(8,128)(2,1)}, bf16[1,384,5120]{2,1,0:T(8,128)(2,1)}, u32[]{:S(2)}, u32[]{:S(2)}) %collective-permute-start.15) | collective-permute-done | bytes 3932192 | tf_op jit(solution)/shard_map/ppermute | solution.py:124
  903.0 13.6 all-reduce.3
  916.7 68.3 %collective-permute-done.16 = bf16[1,384,5120]{2,1,0:T(8,128)(2,1)} collective-permute-done((bf16[1,384,5120]{2,1,0:T(8,128)(2,1)}, bf16[1,384,5120]{2,1,0:T(8,128)(2,1)}, u32[]{:S(2)}, u32[]{:S(2)}) %collective-permute-start.16) | collective-permute-done | bytes 3932192 | tf_op jit(solution)/shard_map/ppermute | solution.py:124
  985.2 62.5 %collective-permute-done.17 = bf16[1,384,5120]{2,1,0:T(8,128)(2,1)} collective-permute-done((bf16[1,384,5120]{2,1,0:T(8,128)(2,1)}, bf16[1,384,5120]{2,1,0:T(8,128)(2,1)}, u32[]{:S(2)}, u32[]{:S(2)}) %collective-permute-start.17) | collective-permute-done | bytes 3932192 | tf_op jit(solution)/shard_map/ppermute | solution.py:124
  1047.6 26.6 %fusion.68 = f32[1280,5120]{1,0:T(8,128)} fusion(bf16[1,384,5120]{2,1,0:T(8,128)(2,1)} %collective-permute-done.17, bf16[1,384,5120]{2,1,0:T(8,128)(2,1)} %collective-permute-done.16, bf16[1,384,5120]{2,1,0:T(8,128)(2,1)} %collective-permute-done.15, bf16[1,384,5120]{2,1,0:T(8,128)(2,1)} %param.13, bf16[1,384,1280]{1,2,0:T(8,128)(2,1)} %get-tuple-element.630, ...), kind=kOutput, calls=%fused_computation.96 | convolution fusion | flops 20211302400 | bytes 45875200 | tf_op jit(solution)/shard_map/nth,ntk->hk/dot_general | solution.py:227
  1075.0 2.2 pad_maximum_fusion.5
  1078.0 36.4 %fusion.85 = bf16[1,384,5120]{2,1,0:T(8,128)(2,1)} fusion(bf16[1,384,5120]{2,1,0:T(8,128)(2,1)S(1)} %copy-done.1, bf16[384,5120]{0,1:T(8,128)(2,1)S(1)} %bitcast.350, bf16[5120,5120]{1,0:T(8,128)(2,1)} %all-gather.6.cloned.1.call-done, f32[5120]{0:T(1024)S(1)} %convert_element_type.338), kind=kOutput, calls=%fused_computation.123 | convolution fusion | flops 20140523520 | bytes 64245760 | tf_op jit(solution)/shard_map/dot_general | solution.py:230
  1117.0 13.2 fusion.150
  1130.2 17.7 %collective-permute-done.20 = bf16[1,384,1792]{1,2,0:T(8,128)(2,1)} collective-permute-done((bf16[1,384,1792]{1,2,0:T(8,128)(2,1)}, bf16[1,384,1792]{1,2,0:T(8,128)(2,1)}, u32[]{:S(2)}, u32[]{:S(2)}) %collective-permute-start.20) | collective-permute-done | bytes 1376288 | tf_op jit(solution)/shard_map/ppermute | solution.py:124
  1148.0 50.0 %collective-permute-done.19 = bf16[1,384,1792]{1,2,0:T(8,128)(2,1)} collective-permute-done((bf16[1,384,1792]{1,2,0:T(8,128)(2,1)S(1)}, bf16[1,384,1792]{1,2,0:T(8,128)(2,1)}, u32[]{:S(2)}, u32[]{:S(2)}) %collective-permute-start.19) | collective-permute-done | bytes 1376288 | tf_op jit(solution)/shard_map/ppermute | solution.py:124
  1197.9 35.4 %fusion.88 = (f32[5120]{0:T(1024)S(1)}, f32[384]{0:T(512)S(1)}, bf16[384,5120]{1,0:T(8,128)(2,1)}) fusion(bf16[1,384,5120]{2,1,0:T(8,128)(2,1)} %param.12, f32[384]{0:T(512)S(1)} %copy-done.19, f32[5120]{0:T(1024)S(1)} %copy-done.17, f32[384,5120]{1,0:T(8,128)} %fusion.150, bf16[5120,5376]{1,0:T(8,128)(2,1)} %all-gather.8.cloned.1.call-done, ...), kind=kOutput, calls=%fused_computation.126 | convolution fusion | flops 21171335168 | bytes 74951680 | tf_op jit(solution)/shard_map/ntc,dc->ntd/dot_general | solution.py:233
  1233.4 7.8 convert_reduce_fusion.1
  1241.2 42.0 %all-reduce.2 = (f32[5120]{0:T(1024)}, f32[5120]{0:T(1024)}) all-reduce(f32[5120]{0:T(1024)S(1)} %get-tuple-element.568, f32[5120]{0:T(1024)S(1)} %get-tuple-element.627), channel_id=1, replica_groups=mesh['tp'=4,'fsdp'=8] {'fsdp','tp'}, use_global_device_ids=true, to_apply=%region_14.15 | all-reduce | flops 10240 | bytes 81920 | tf_op jit(solution)/shard_map/psum | solution.py:235
  1283.3 175.4 %reduce-scatter.3.cloned.1.call-done = f32[640,1792]{1,0:T(8,128)} async-done(((f32[5120,1792]{1,0:T(8,128)}), f32[640,1792]{1,0:T(8,128)}) %reduce-scatter.3.cloned.1.call-update) | async-done | bytes 4587536 | tf_op jit(solution)/shard_map/reduce_scatter | solution.py:218
  (380 shorter events, 199.9 us)
Async XLA Ops:
  7.2 287.2 %all-gather.4.cloned.1.call-start = ((), (), s32[]{:S(2)}) async-start(), calls=%async_computation.2 | async-start | bytes 20643840 | tf_op jit(solution)/shard_map/all_gather | solution.py:173
  7.9 389.4 %all-gather.6.cloned.1.call-start = ((), (), s32[]{:S(2)}) async-start(), calls=%async_computation.3 | async-start | bytes 58982400 | tf_op jit(solution)/shard_map/all_gather | solution.py:175
  7.9 41.1 %collective-permute-start = (bf16[160,5120]{1,0:T(8,128)(2,1)}, bf16[160,5120]{1,0:T(8,128)(2,1)S(1)}, u32[]{:S(2)}, u32[]{:S(2)}) collective-permute-start(bf16[160,5120]{1,0:T(8,128)(2,1)} %param.18), channel_id=1, source_target_pairs={{0,8},{8,16},{16,24},{24,0},{1,9},{9,17},{17,25},{25,1},{2,10},{10... | collective-permute-start | bytes 4915208 | tf_op jit(solution)/shard_map/ppermute | solution.py:124
  49.1 38.8 %collective-permute-start.1 = (bf16[160,5120]{1,0:T(8,128)(2,1)S(1)}, bf16[160,5120]{1,0:T(8,128)(2,1)S(1)}, u32[]{:S(2)}, u32[]{:S(2)}) collective-permute-start(bf16[160,5120]{1,0:T(8,128)(2,1)S(1)} %collective-permute-done), channel_id=1, source_target_pairs={{0,8},{8,16},{16,24},{24,0},{1,9},{9,17},{17,25},{25,1},{2,10},{10... | collective-permute-start | bytes 4915208 | tf_op jit(solution)/shard_map/ppermute | solution.py:124
  87.8 37.9 %collective-permute-start.2 = (bf16[160,5120]{1,0:T(8,128)(2,1)S(1)}, bf16[160,5120]{1,0:T(8,128)(2,1)S(1)}, u32[]{:S(2)}, u32[]{:S(2)}) collective-permute-start(bf16[160,5120]{1,0:T(8,128)(2,1)S(1)} %collective-permute-done.1), channel_id=1, source_target_pairs={{0,8},{8,16},{16,24},{24,0},{1,9},{9,17},{17,25},{25,1},{2,10},{10... | collective-permute-start | bytes 4915208 | tf_op jit(solution)/shard_map/ppermute | solution.py:124
  130.5 1.6 copy-start.11
  130.5 999.7 %all-gather.8.cloned.1.call-start = ((), (), s32[]{:S(2)}) async-start(), calls=%async_computation.4 | async-start | bytes 61931520 | tf_op jit(solution)/shard_map/all_gather | solution.py:177
  132.1 51.1 %collective-permute-start.3 = (bf16[640,1792]{1,0:T(8,128)(2,1)S(1)}, bf16[640,1792]{1,0:T(8,128)(2,1)S(1)}, u32[]{:S(2)}, u32[]{:S(2)}) collective-permute-start(bf16[640,1792]{1,0:T(8,128)(2,1)S(1)} %copy-done.11), channel_id=1, source_target_pairs={{0,8},{8,16},{16,24},{24,0},{1,9},{9,17},{17,25},{25,1},{2,10},{10... | collective-permute-start | bytes 6881288 | tf_op jit(solution)/shard_map/ppermute | solution.py:124
  183.2 50.2 %collective-permute-start.4 = (bf16[640,1792]{1,0:T(8,128)(2,1)S(1)}, bf16[640,1792]{1,0:T(8,128)(2,1)S(1)}, u32[]{:S(2)}, u32[]{:S(2)}) collective-permute-start(bf16[640,1792]{1,0:T(8,128)(2,1)S(1)} %collective-permute-done.3), channel_id=1, source_target_pairs={{0,8},{8,16},{16,24},{24,0},{1,9},{9,17},{17,25},{25,1},{2,10},{10... | collective-permute-start | bytes 6881288 | tf_op jit(solution)/shard_map/ppermute | solution.py:124
  233.5 49.4 %collective-permute-start.5 = (bf16[640,1792]{1,0:T(8,128)(2,1)S(1)}, bf16[640,1792]{1,0:T(8,128)(2,1)S(1)}, u32[]{:S(2)}, u32[]{:S(2)}) collective-permute-start(bf16[640,1792]{1,0:T(8,128)(2,1)S(1)} %collective-permute-done.4), channel_id=1, source_target_pairs={{0,8},{8,16},{16,24},{24,0},{1,9},{9,17},{17,25},{25,1},{2,10},{10... | collective-permute-start | bytes 6881288 | tf_op jit(solution)/shard_map/ppermute | solution.py:124
  286.0 3.2 copy-start.16
  286.0 997.2 %reduce-scatter.5.cloned.1.call-start = ((), (), s32[]{:S(2)}) async-start(), calls=%async_computation.6 | async-start | bytes 29491200 | tf_op jit(solution)/shard_map/reduce_scatter | solution.py:228
  286.1 3.3 copy-start
  289.4 3.2 copy-start.18
  289.4 3.4 copy-start.21
  289.4 3.4 copy-start.22
  292.6 84.1 %collective-permute-start.6 = (bf16[1,384,5120]{2,1,0:T(8,128)(2,1)}, bf16[1,384,5120]{2,1,0:T(8,128)(2,1)}, u32[]{:S(2)}, u32[]{:S(2)}) collective-permute-start(bf16[1,384,5120]{2,1,0:T(8,128)(2,1)} %fusion.77), channel_id=1, source_target_pairs={{0,8},{8,16},{16,24},{24,0},{1,9},{9,17},{17,25},{25,1},{2,10},{10... | collective-permute-start | bytes 11796488 | tf_op jit(solution)/shard_map/ppermute | solution.py:124
  397.1 85.3 %collective-permute-start.7 = (bf16[1,384,5120]{2,1,0:T(8,128)(2,1)}, bf16[1,384,5120]{2,1,0:T(8,128)(2,1)}, u32[]{:S(2)}, u32[]{:S(2)}) collective-permute-start(bf16[1,384,5120]{2,1,0:T(8,128)(2,1)} %collective-permute-done.6), channel_id=1, source_target_pairs={{0,8},{8,16},{16,24},{24,0},{1,9},{9,17},{17,25},{25,1},{2,10},{10... | collective-permute-start | bytes 11796488 | tf_op jit(solution)/shard_map/ppermute | solution.py:124
  482.4 4.0 copy-start.5
  482.4 78.7 %collective-permute-start.8 = (bf16[1,384,5120]{2,1,0:T(8,128)(2,1)}, bf16[1,384,5120]{2,1,0:T(8,128)(2,1)}, u32[]{:S(2)}, u32[]{:S(2)}) collective-permute-start(bf16[1,384,5120]{2,1,0:T(8,128)(2,1)} %collective-permute-done.7), channel_id=1, source_target_pairs={{0,8},{8,16},{16,24},{24,0},{1,9},{9,17},{17,25},{25,1},{2,10},{10... | collective-permute-start | bytes 11796488 | tf_op jit(solution)/shard_map/ppermute | solution.py:124
  594.1 60.5 %collective-permute-start.9 = (bf16[1,384,1280]{1,2,0:T(8,128)(2,1)}, bf16[1,384,1280]{1,2,0:T(8,128)(2,1)}, u32[]{:S(2)}, u32[]{:S(2)}) collective-permute-start(bf16[1,384,1280]{1,2,0:T(8,128)(2,1)} %bitcast.360), channel_id=1, source_target_pairs={{0,8},{8,16},{16,24},{24,0},{1,9},{9,17},{17,25},{25,1},{2,10},{10... | collective-permute-start | bytes 2949128 | tf_op jit(solution)/shard_map/ppermute | solution.py:124
  594.1 60.5 %collective-permute-start.10 = (bf16[1,384,1280]{1,2,0:T(8,128)(2,1)}, bf16[1,384,1280]{1,2,0:T(8,128)(2,1)}, u32[]{:S(2)}, u32[]{:S(2)}) collective-permute-start(bf16[1,384,1280]{1,2,0:T(8,128)(2,1)} %bitcast.359), channel_id=1, source_target_pairs={{0,16},{8,24},{16,0},{24,8},{1,17},{9,25},{17,1},{25,9},{2,18},{10... | collective-permute-start | bytes 2949128 | tf_op jit(solution)/shard_map/ppermute | solution.py:124
  594.1 60.5 %collective-permute-start.11 = (bf16[1,384,1280]{1,2,0:T(8,128)(2,1)}, bf16[1,384,1280]{1,2,0:T(8,128)(2,1)}, u32[]{:S(2)}, u32[]{:S(2)}) collective-permute-start(bf16[1,384,1280]{1,2,0:T(8,128)(2,1)} %bitcast.358), channel_id=1, source_target_pairs={{0,24},{8,0},{16,8},{24,16},{1,25},{9,1},{17,9},{25,17},{2,26},{10... | collective-permute-start | bytes 2949128 | tf_op jit(solution)/shard_map/ppermute | solution.py:124
  649.2 2.4 copy-start.2
  654.6 210.1 %collective-permute-start.14 = (bf16[1,384,1280]{1,2,0:T(8,128)(2,1)}, bf16[1,384,1280]{1,2,0:T(8,128)(2,1)}, u32[]{:S(2)}, u32[]{:S(2)}) collective-permute-start(bf16[1,384,1280]{1,2,0:T(8,128)(2,1)} %get-tuple-element.483), channel_id=1, source_target_pairs={{0,24},{8,0},{16,8},{24,16},{1,25},{9,1},{17,9},{25,17},{2,26},{10... | collective-permute-start | bytes 2949128 | tf_op jit(solution)/shard_map/ppermute | solution.py:124
  695.5 169.2 %collective-permute-start.13 = (bf16[1,384,1280]{1,2,0:T(8,128)(2,1)}, bf16[1,384,1280]{1,2,0:T(8,128)(2,1)}, u32[]{:S(2)}, u32[]{:S(2)}) collective-permute-start(bf16[1,384,1280]{1,2,0:T(8,128)(2,1)} %get-tuple-element.482), channel_id=1, source_target_pairs={{0,16},{8,24},{16,0},{24,8},{1,17},{9,25},{17,1},{25,9},{2,18},{10... | collective-permute-start | bytes 2949128 | tf_op jit(solution)/shard_map/ppermute | solution.py:124
  695.5 169.2 %collective-permute-start.12 = (bf16[1,384,1280]{1,2,0:T(8,128)(2,1)}, bf16[1,384,1280]{1,2,0:T(8,128)(2,1)}, u32[]{:S(2)}, u32[]{:S(2)}) collective-permute-start(bf16[1,384,1280]{1,2,0:T(8,128)(2,1)} %get-tuple-element.481), channel_id=1, source_target_pairs={{0,8},{8,16},{16,24},{24,0},{1,9},{9,17},{17,25},{25,1},{2,10},{10... | collective-permute-start | bytes 2949128 | tf_op jit(solution)/shard_map/ppermute | solution.py:124
  700.3 5.1 copy-start.4
  814.7 85.3 %collective-permute-start.15 = (bf16[1,384,5120]{2,1,0:T(8,128)(2,1)}, bf16[1,384,5120]{2,1,0:T(8,128)(2,1)}, u32[]{:S(2)}, u32[]{:S(2)}) collective-permute-start(bf16[1,384,5120]{2,1,0:T(8,128)(2,1)} %param.13), channel_id=1, source_target_pairs={{0,8},{8,16},{16,24},{24,0},{1,9},{9,17},{17,25},{25,1},{2,10},{10... | collective-permute-start | bytes 11796488 | tf_op jit(solution)/shard_map/ppermute | solution.py:124
  819.6 0.7 copy-start.7
  819.6 3.5 copy-start.9
  823.1 1.4 copy-start.3
  828.4 71.6 %copy-start.8 = (bf16[1,1536,2,64]{1,3,2,0:T(8,128)(2,1)S(1)}, bf16[1,1536,2,64]{1,3,2,0:T(8,128)(2,1)}, u32[]{:S(2)}) copy-start(bf16[1,1536,2,64]{1,3,2,0:T(8,128)(2,1)} %copy-done.7) | copy-start | bytes 1179652
  828.4 71.6 %copy-start.10 = (bf16[1,1536,2,64]{1,3,2,0:T(8,128)(2,1)S(1)}, bf16[1,1536,2,64]{1,3,2,0:T(8,128)(2,1)}, u32[]{:S(2)}) copy-start(bf16[1,1536,2,64]{1,3,2,0:T(8,128)(2,1)} %copy-done.9) | copy-start | bytes 1179652
  900.0 84.9 %collective-permute-start.16 = (bf16[1,384,5120]{2,1,0:T(8,128)(2,1)}, bf16[1,384,5120]{2,1,0:T(8,128)(2,1)}, u32[]{:S(2)}, u32[]{:S(2)}) collective-permute-start(bf16[1,384,5120]{2,1,0:T(8,128)(2,1)} %collective-permute-done.15), channel_id=1, source_target_pairs={{0,8},{8,16},{16,24},{24,0},{1,9},{9,17},{17,25},{25,1},{2,10},{10... | collective-permute-start | bytes 11796488 | tf_op jit(solution)/shard_map/ppermute | solution.py:124
  901.9 145.7 %copy-start.6 = (bf16[1,384,1280]{1,2,0:T(8,128)(2,1)S(1)}, bf16[1,384,1280]{1,2,0:T(8,128)(2,1)}, u32[]{:S(2)}) copy-start(bf16[1,384,1280]{1,2,0:T(8,128)(2,1)} %get-tuple-element.480) | copy-start | bytes 2949124
  901.9 145.7 %copy-start.15 = (bf16[1,384,1280]{1,2,0:T(8,128)(2,1)S(1)}, bf16[1,384,1280]{1,2,0:T(8,128)(2,1)}, u32[]{:S(2)}) copy-start(bf16[1,384,1280]{1,2,0:T(8,128)(2,1)} %get-tuple-element.629) | copy-start | bytes 2949124
  985.0 62.7 %collective-permute-start.17 = (bf16[1,384,5120]{2,1,0:T(8,128)(2,1)}, bf16[1,384,5120]{2,1,0:T(8,128)(2,1)}, u32[]{:S(2)}, u32[]{:S(2)}) collective-permute-start(bf16[1,384,5120]{2,1,0:T(8,128)(2,1)} %collective-permute-done.16), channel_id=1, source_target_pairs={{0,8},{8,16},{16,24},{24,0},{1,9},{9,17},{17,25},{25,1},{2,10},{10... | collective-permute-start | bytes 11796488 | tf_op jit(solution)/shard_map/ppermute | solution.py:124
  1074.3 384.4 %reduce-scatter.3.cloned.1.call-start = ((), (), s32[]{:S(2)}) async-start(), calls=%async_computation.5 | async-start | bytes 41287680 | tf_op jit(solution)/shard_map/reduce_scatter | solution.py:218
  1075.0 3.0 copy-start.1
  1078.0 38.2 %copy-start.13 = (bf16[1,384,1792]{1,2,0:T(8,128)(2,1)S(1)}, bf16[1,384,1792]{1,2,0:T(8,128)(2,1)}, u32[]{:S(2)}) copy-start(bf16[1,384,1792]{1,2,0:T(8,128)(2,1)} %get-tuple-element.494) | copy-start | bytes 4128772
  1078.0 38.2 %copy-start.12 = (bf16[1,384,1792]{1,2,0:T(8,128)(2,1)S(1)}, bf16[1,384,1792]{1,2,0:T(8,128)(2,1)}, u32[]{:S(2)}) copy-start(bf16[1,384,1792]{1,2,0:T(8,128)(2,1)} %get-tuple-element.493) | copy-start | bytes 4128772
  1078.0 39.0 %copy-start.14 = (bf16[1,384,1792]{1,2,0:T(8,128)(2,1)S(1)}, bf16[1,384,1792]{1,2,0:T(8,128)(2,1)}, u32[]{:S(2)}) copy-start(bf16[1,384,1792]{1,2,0:T(8,128)(2,1)} %get-tuple-element.492) | copy-start | bytes 4128772
  1114.4 83.6 %copy-start.17 = (f32[5120]{0:T(1024)S(1)}, f32[5120]{0:T(1024)}, u32[]{:S(2)}) copy-start(f32[5120]{0:T(1024)} %param.14) | copy-start | bytes 61444
  1114.4 83.6 %copy-start.19 = (f32[384]{0:T(512)S(1)}, f32[384]{0:T(512)}, u32[]{:S(2)}) copy-start(f32[384]{0:T(512)} %copy-done.18) | copy-start | bytes 4612
  1114.4 33.6 %collective-permute-start.20 = (bf16[1,384,1792]{1,2,0:T(8,128)(2,1)}, bf16[1,384,1792]{1,2,0:T(8,128)(2,1)}, u32[]{:S(2)}, u32[]{:S(2)}) collective-permute-start(bf16[1,384,1792]{1,2,0:T(8,128)(2,1)} %get-tuple-element.495), channel_id=1, source_target_pairs={{0,24},{8,0},{16,8},{24,16},{1,25},{9,1},{17,9},{25,17},{2,26},{10... | collective-permute-start | bytes 4128776 | tf_op jit(solution)/shard_map/ppermute | solution.py:124
  1116.1 81.8 %collective-permute-start.19 = (bf16[1,384,1792]{1,2,0:T(8,128)(2,1)S(1)}, bf16[1,384,1792]{1,2,0:T(8,128)(2,1)}, u32[]{:S(2)}, u32[]{:S(2)}) collective-permute-start(bf16[1,384,1792]{1,2,0:T(8,128)(2,1)S(1)} %copy-done.13), channel_id=1, source_target_pairs={{0,16},{8,24},{16,0},{24,8},{1,17},{9,25},{17,1},{25,9},{2,18},{10... | collective-permute-start | bytes 4128776 | tf_op jit(solution)/shard_map/ppermute | solution.py:124
  1116.1 81.8 %collective-permute-start.18 = (bf16[1,384,1792]{1,2,0:T(8,128)(2,1)S(1)}, bf16[1,384,1792]{1,2,0:T(8,128)(2,1)}, u32[]{:S(2)}, u32[]{:S(2)}) collective-permute-start(bf16[1,384,1792]{1,2,0:T(8,128)(2,1)S(1)} %copy-done.12), channel_id=1, source_target_pairs={{0,8},{8,16},{16,24},{24,0},{1,9},{9,17},{17,25},{25,1},{2,10},{10... | collective-permute-start | bytes 4128776 | tf_op jit(solution)/shard_map/ppermute | solution.py:124
  (1 other events, 0.7 us)
Sparse Core Ops, SparseCore 0:
  9.9 99.0 all-gather.3
  130.6 238.6 all-gather.5
  371.2 251.7 all-gather.7
  1074.4 159.9 reduce-scatter.4
  1238.6 220.0 reduce-scatter.2
